TPU v7x, 32 devices: a whole 2x2x4 slice. The times are simulated.
32 devices in a mesh: lat: 8 (over z, core), rad: 4 (over y, x).
Axes of the slice: x: 2, y: 2, z: 4, core: 2. Of those that a mesh axis runs over, the one named last changes fastest.
Arguments:
- residual: float32 [3, 32, 64, 256], P(None, 'rad', 'lat'), may hold values from -30 to 30
- prev_basis: float32 [4, 3, 32, 64, 256], P(None, None, 'rad', 'lat'), may hold values from -30 to 30
- layer_ids: int32 [16, 32, 128], P('rad', 'lat'), may hold values from 0 to 7
- viscosity: float32 [8], replicated, may hold values from 0.1 to 1
- shifts: float32 [4], replicated, may hold values from 0.3 to 2
Outputs:
- new_basis: float32 [4, 3, 32, 64, 256], P(None, None, 'rad', 'lat')
- gram_matrix: float32 [9, 9], replicated
All inputs are finite; a program needn't handle non-finite values.
Results may differ from a plain program's by a relative error of at most 0.00019.
Values sent between devices are 32-bit elements; how exact they have to be, the bound alone decides.
A program may use at most 128 MiB of HBM per device.

v0:
```python
import functools

import jax
import jax.numpy as jnp
from jax import lax
from jax.experimental import pallas as pl
from jax.experimental.pallas import tpu as pltpu
from jax.sharding import PartitionSpec as P

MESH = pl.DeviceIdType.MESH
F32 = jnp.float32

mass = (1.0 / 36, 1.0 / 12, 1.0 / 45)
stiff = (0.0, 1.0, 4.0 / 3)

DIRS = ((-1, -1), (-1, 0), (-1, 1), (0, -1), (0, 1), (1, -1), (1, 0), (1, 1))
SLOT = {d: i for i, d in enumerate(DIRS)}
R_DIRS = {(-1, 0): 0, (1, 0): 1}
X_DIRS = {(0, -1): 0, (0, 1): 1}
C_DIRS = {(-1, -1): 0, (-1, 1): 1, (1, -1): 2, (1, 1): 3}
FIRST = ((-1, 0), (0, -1), (-1, -1))
LAST = ((1, 0), (0, 1), (1, 1))


def weight(a, b, c):
    return (
        stiff[a] * mass[b] * mass[c] + mass[a] * stiff[b] * mass[c] + mass[a] * mass[b] * stiff[c]
    )


def forward(u0, u1, u2):
    total = u0 + u2
    twice = u1 + u1
    return total + (twice + twice), u0 - u2, total - twice


def backward(m0, m1, m2):
    both = m0 + m2
    half = m0 + m0 - m2
    return both + m1, half + half, both - m1


def kernel(
    n_lat,
    n_rad,
    n_steps,
    n_prev,
    comps,
    res_ref,
    prev_ref,
    ids_hbm,
    visc_hbm,
    shift_hbm,
    out_ref,
    gram_ref,
    stage,
    ids_ref,
    visc_ref,
    shift_ref,
    work,
    vec,
    ghost_r,
    ghost_x,
    ghost_c,
    scaled,
    send_r,
    send_x,
    send_c,
    recv_r,
    recv_x,
    recv_c,
    gram_send,
    gram_recv,
    in_sem,
    send_sem,
    recv_sem,
    gram_sems,
):
    n_dev = n_lat * n_rad
    lat = lax.axis_index("lat")
    rad = lax.axis_index("rad")
    me = lat * n_rad + rad
    rows = res_ref.shape[0]
    half_y = res_ref.shape[1] // 2
    n_vec = n_prev + n_steps + 1

    res_copy = pltpu.make_async_copy(res_ref, stage.at[n_prev], in_sem.at[0])
    res_copy.start()
    prev_copy = pltpu.make_async_copy(prev_ref, stage.at[pl.ds(0, n_prev)], in_sem.at[1])
    small_copies = [
        pltpu.make_async_copy(a, b, in_sem.at[2 + i])
        for i, (a, b) in enumerate(
            ((ids_hbm, ids_ref), (visc_hbm, visc_ref), (shift_hbm, shift_ref))
        )
    ]
    for copy in small_copies:
        copy.start()
    prev_copy.start()

    recv_r[...] = jnp.zeros_like(recv_r)
    recv_x[...] = jnp.zeros_like(recv_x)
    recv_c[...] = jnp.zeros_like(recv_c)

    barrier = pltpu.get_barrier_semaphore()

    rad_targets = [lax.rem(rad + d, n_rad) for d in range(n_rad)]

    def each_other(visit):
        def row(ahead, carry):
            lat_target = lax.rem(lat + ahead, n_lat)
            for d in range(n_rad):
                visit(ahead * n_rad + d - 1, {"lat": lat_target, "rad": rad_targets[d]})
            return carry

        lax.fori_loop(1, n_lat, row, 0, unroll=n_lat <= 8)
        for d in range(1, n_rad):
            visit(d - 1, {"lat": lat, "rad": rad_targets[d]})

    def greet(slot, device):
        pl.semaphore_signal(barrier, inc=1, device_id=device, device_id_type=MESH)

    each_other(greet)

    sub = lax.broadcasted_iota(jnp.int32, (8, half_y), 0)
    lane = lax.broadcasted_iota(jnp.int32, (8, half_y), 1)
    upper = sub >= 4
    ex = lax.rem(sub, 4)
    first_x = ex == 0
    last_x = ex == 3
    corner0 = sub == 0
    corner3 = sub == 3
    corner4 = sub == 4
    corner7 = sub == 7
    has_up = rad < n_rad - 1
    has_right = lat < n_lat - 1
    up_f = jnp.where(has_up, 1.0, 0.0).astype(F32)
    right_f = jnp.where(has_right, 1.0, 0.0).astype(F32)
    both_f = up_f * right_f

    def roll_s(v, k):
        return pltpu.roll(v, k % 8, 0)

    def keep(mask, v):
        return jnp.where(mask, v, 0.0)

    src = lax.broadcasted_iota(jnp.int32, (2 * half_y, 2 * half_y), 0)
    dst = lax.broadcasted_iota(jnp.int32, (2 * half_y, 2 * half_y), 1)
    split_perm = jnp.where(
        src == jnp.where(dst < half_y, 2 * dst, 2 * (dst - half_y) + 1), 1.0, 0.0
    ).astype(F32)
    join_perm = jnp.where(
        dst == jnp.where(src < half_y, 2 * src, 2 * (src - half_y) + 1), 1.0, 0.0
    ).astype(F32)

    def exact_dot(a, b):
        return jnp.dot(a, b, precision=lax.Precision.HIGHEST, preferred_element_type=F32)

    def split_columns(i):
        z = exact_dot(stage[i], split_perm)
        work[i, 0] = z[:, :half_y]
        work[i, 1] = z[:, half_y:]

    def native(c, ro, p, h):
        return pl.ds(c * 64 + (4 * h + ro) * 8 + p, 4, stride=2)

    kinds = {}
    for a in range(3):
        for b in range(3):
            for c in range(3):
                key = tuple(sorted((a, b, c)))
                if key != (0, 0, 0) and key not in kinds:
                    kinds[key] = len(kinds)
    def copy_of(step, c, d):
        if d in R_DIRS:
            a, b = send_r.at[step, c, R_DIRS[d]], recv_r.at[step, c, R_DIRS[d]]
        elif d in X_DIRS:
            a, b = send_x.at[step, c, X_DIRS[d]], recv_x.at[step, c, X_DIRS[d]]
        else:
            a, b = send_c.at[step, c, C_DIRS[d]], recv_c.at[step, c, C_DIRS[d]]
        return pltpu.make_async_remote_copy(
            src_ref=a,
            dst_ref=b,
            send_sem=send_sem.at[step, c, SLOT[d]],
            recv_sem=recv_sem.at[step, c, SLOT[d]],
            device_id={"lat": lat + d[1], "rad": rad + d[0]},
            device_id_type=MESH,
        )

    def inside(dr, dx):
        ok = None
        for pos, step, count in ((rad, dr, n_rad), (lat, dx, n_lat)):
            if step:
                one = (pos > 0) if step < 0 else (pos < count - 1)
                ok = one if ok is None else jnp.logical_and(ok, one)
        return ok

    order = ((-1, -1), (1, 1), (-1, 1), (1, -1), (1, 0), (-1, 0), (0, 1), (0, -1))

    def dirs_of(step):
        wanted = FIRST if step == 0 else (LAST if step == n_steps else DIRS)
        return [d for d in order if d in wanted]

    def start_round(step, c):
        for d in dirs_of(step):

            @pl.when(inside(*d))
            def _(d=d):
                copy_of(step, c, d).start()

    def finish_round(step, c):
        for d in dirs_of(step):

            @pl.when(inside(-d[0], -d[1]))
            def _(d=d):
                copy_of(step, c, d).wait_recv()

    def pack_x(vals, at):
        out = None
        for ro in range(4):
            moved = roll_s(vals[ro], ro - at)
            out = moved if out is None else jnp.where(ex == ro, moved, out)
        return out

    def apply(k, c):
        s = shift_ref[k]
        cur = k % 2
        new = 1 - cur
        u = {}
        gx = {}
        for q in range(2):
            for ro in range(4):
                gx[ro, q] = ghost_x[cur, c, ro, q]
                for p in range(2):
                    u[ro, p, q] = vec[cur, c, ro, p, q]
            gx[4, q] = jnp.where(upper, ghost_c[cur, c, q], roll_s(gx[0, q], 4))
            for p in range(2):
                u[4, p, q] = jnp.where(upper, ghost_r[cur, c, p, q], roll_s(u[0, p, q], 4))
            for ro in range(5):
                u[ro, 2, q] = jnp.where(last_x, gx[ro, q], roll_s(u[ro, 0, q], -1))
        res = {}
        for e in range(2):
            t = {}
            for p in range(3):
                for q in range(2):
                    t[0, p, q], t[1, p, q], t[2, p, q] = forward(
                        u[2 * e, p, q], u[2 * e + 1, p, q], u[2 * e + 2, p, q]
                    )
            w = {}
            for a in range(3):
                x = {}
                for q in range(2):
                    x[0, q], x[1, q], x[2, q] = forward(t[a, 0, q], t[a, 1, q], t[a, 2, q])
                for b in range(3):
                    nxt = keep(lane != half_y - 1, pltpu.roll(x[b, 0], half_y - 1, 1))
                    m = list(forward(x[b, 0], x[b, 1], nxt))
                    for j in range(3):
                        key = tuple(sorted((a, b, j)))
                        if key in kinds:
                            m[j] = m[j] * scaled[e, kinds[key]]
                        else:
                            m[j] = None
                    if m[0] is None:
                        r0 = m[1] + m[2]
                        r1 = -(m[2] + m[2])
                        r2 = m[2] - m[1]
                    else:
                        r0, r1, r2 = backward(*m)
                    x[b, 0] = r0 + keep(lane != 0, pltpu.roll(r2, 1, 1))
                    x[b, 1] = r1
                for q in range(2):
                    w[a, 0, q], w[a, 1, q], w[a, 2, q] = backward(x[0, q], x[1, q], x[2, q])
            for p in range(3):
                for q in range(2):
                    r = backward(w[0, p, q], w[1, p, q], w[2, p, q])
                    for i in range(3):
                        key = (2 * e + i, p, q)
                        res[key] = res[key] + r[i] if key in res else r[i]
        px = {}
        for q in range(2):
            for ro in range(5):
                edge = res[ro, 2, q]
                px[ro, q] = edge
                res[ro, 0, q] = res[ro, 0, q] + keep(ex != 0, roll_s(edge, 1))
            for p in range(2):
                res[0, p, q] = res[0, p, q] + keep(upper, roll_s(res[4, p, q], 4))
            px[0, q] = px[0, q] + keep(upper, roll_s(px[4, q], 4))
        step = k + 1
        last = step == n_steps
        for q in range(2):
            face = slice(8 * q, 8 * q + 8)
            edge = slice(16 + q, 17 + q)
            row = slice(q, q + 1)
            send_r[step, c, 1, face] = jnp.where(upper, res[4, 1, q], roll_s(res[4, 0, q], 4))
            send_r[step, c, 1, edge] = px[4, q][7:8]
            send_x[step, c, 1, face] = pack_x([px[ro, q] for ro in range(4)], 3)
            send_x[step, c, 1, edge] = px[4, q][7:8]
            send_c[step, c, 3, row] = px[4, q][7:8]
            if not last:
                send_r[step, c, 0, face] = jnp.where(upper, roll_s(res[0, 1, q], 4), res[0, 0, q])
                send_r[step, c, 0, edge] = px[0, q][3:4]
                send_x[step, c, 0, face] = pack_x([res[ro, 0, q] for ro in range(4)], 0)
                send_x[step, c, 0, edge] = res[4, 0, q][4:5]
                send_c[step, c, 0, row] = res[0, 0, q][0:1]
                send_c[step, c, 1, row] = px[0, q][3:4]
                send_c[step, c, 2, row] = res[4, 0, q][4:5]
            for ro in range(4):
                for p in range(2):
                    vec[new, c, ro, p, q] = res[ro, p, q] - s * u[ro, p, q]
                if not last:
                    ghost_x[new, c, ro, q] = px[ro, q] - s * gx[ro, q]
            if not last:
                for p in range(2):
                    ghost_r[new, c, p, q] = res[4, p, q] - s * u[4, p, q]
                ghost_c[new, c, q] = px[4, q] - s * gx[4, q]

    def absorb(step, c):
        new = step % 2
        first, last = step == 0, step == n_steps
        for q in range(2):
            face = slice(8 * q, 8 * q + 8)
            line = slice(16 + q, 17 + q)
            row = slice(q, q + 1)

            def spot(ref_row, mask):
                return keep(mask, jnp.broadcast_to(ref_row, (8, half_y)))

            if not first:
                from_low = recv_r[step, c, 1, face]
                from_left = recv_x[step, c, 1, face]
                corner = spot(recv_c[step, c, 3, row], corner0)
                vec[new, c, 0, 0, q] += (
                    keep(~upper, from_low) + keep(first_x, from_left) + corner
                )
                vec[new, c, 0, 1, q] += keep(~upper, roll_s(from_low, 4))
                for ro in range(1, 4):
                    vec[new, c, ro, 0, q] += keep(first_x, roll_s(from_left, -ro))
            if not last:
                from_up = recv_r[step, c, 0, face]
                from_right = recv_x[step, c, 0, face]
                add0 = keep(upper, roll_s(from_up, 4))
                add1 = keep(upper, from_up)
                edge = keep(last_x, roll_s(from_right, 3))
                far = (
                    spot(recv_r[step, c, 0, line], corner7)
                    + spot(recv_x[step, c, 0, line], corner7)
                    + spot(recv_c[step, c, 0, row], corner7)
                )
                if not first:
                    add0 = (
                        add0
                        + spot(recv_x[step, c, 1, line], corner4)
                        + spot(recv_c[step, c, 1, row], corner4)
                    )
                    edge = (
                        edge
                        + spot(recv_r[step, c, 1, line], corner3)
                        + spot(recv_c[step, c, 2, row], corner3)
                    )
                    add0 = add0 + ghost_r[new, c, 0, q]
                    add1 = add1 + ghost_r[new, c, 1, q]
                    edge = edge + ghost_x[new, c, 0, q]
                    far = far + ghost_c[new, c, q]
                ghost_r[new, c, 0, q] = add0 * up_f
                ghost_r[new, c, 1, q] = add1 * up_f
                ghost_x[new, c, 0, q] = edge * right_f
                ghost_c[new, c, q] = far * both_f
                for ro in range(1, 4):
                    edge = keep(last_x, roll_s(from_right, 3 - ro))
                    if not first:
                        edge = edge + ghost_x[new, c, ro, q]
                    ghost_x[new, c, ro, q] = edge * right_f

    def to_native(k):
        cur = k % 2
        for c in range(comps):
            for ro in range(4):
                for p in range(2):
                    for q in range(2):
                        v = vec[cur, c, ro, p, q]
                        for h in range(2):
                            work[n_prev + k, q, native(c, ro, p, h), :] = v[4 * h : 4 * h + 4]

    def write_out(k):
        z = jnp.concatenate([work[n_prev + k, 0], work[n_prev + k, 1]], 1)
        out_ref[k - 1] = exact_dot(z, join_perm)

    lane16 = lax.broadcasted_iota(jnp.int32, (16, half_y), 1)
    row16 = lax.broadcasted_iota(jnp.int32, (16, half_y), 0)

    def gram_row(i):
        def chunk(t, acc):
            at = pl.ds(pl.multiple_of(8 * t, 8), 8)
            for q in range(2):
                mine = work[i, q, at, :]
                acc = tuple(
                    acc[j] + mine * (mine if j == i else work[j, q, at, :]) for j in range(i + 1)
                )
            return acc

        acc = lax.fori_loop(
            0, rows // 8, chunk, (jnp.zeros((8, half_y), F32),) * (i + 1), unroll=4
        )
        sums = [jnp.sum(a, axis=0, keepdims=True) for a in acc]
        sums.append(jnp.zeros((16 - len(sums), half_y), F32))
        total = jnp.sum(jnp.concatenate(sums, 0), axis=1, keepdims=True)
        hit = jnp.logical_or(lane16 == i * n_vec + row16, lane16 == row16 * n_vec + i)
        hit = jnp.logical_and(hit, row16 <= i)
        return jnp.sum(jnp.where(hit, jnp.broadcast_to(total, hit.shape), 0.0), 0, keepdims=True)

    res_copy.wait()
    split_columns(n_prev)
    for c in range(comps):
        for ro in range(4):
            for p in range(2):
                for q in range(2):
                    vec[0, c, ro, p, q] = jnp.concatenate(
                        [work[n_prev, q, native(c, ro, p, h), :] for h in range(2)], 0
                    )
    zero_rows = jnp.zeros((2, half_y), F32)
    for c in range(comps):
        send_r[0, c, 0, 16:18] = zero_rows
        send_x[0, c, 0, 16:18] = zero_rows
        for q in range(2):
            face = slice(8 * q, 8 * q + 8)
            send_r[0, c, 0, face] = jnp.where(
                upper, roll_s(vec[0, c, 0, 1, q], 4), vec[0, c, 0, 0, q]
            )
            send_x[0, c, 0, face] = pack_x([vec[0, c, ro, 0, q] for ro in range(4)], 0)
            send_c[0, c, 0, q : q + 1] = vec[0, c, 0, 0, q, 0:1]

    pl.semaphore_wait(barrier, n_dev - 1)
    for c in range(comps):
        start_round(0, c)
    for copy in small_copies:
        copy.wait()
    for e in range(2):
        ids = jnp.concatenate([ids_ref[e], ids_ref[2 + e]], 0)
        eta = jnp.zeros((8, half_y), F32)
        for layer in range(visc_ref.shape[0]):
            eta = eta + jnp.where(ids == layer, visc_ref[layer], 0.0)
        for key, i in kinds.items():
            scaled[e, i] = eta * weight(*key)
    prev_copy.wait()
    for i in range(n_prev):
        split_columns(i)

    total = jnp.zeros((1, half_y), F32)
    for k in range(n_steps):
        for c in range(comps):
            finish_round(k, c)
            absorb(k, c)
            apply(k, c)
            start_round(k + 1, c)
        if k == 0:
            for i in range(n_prev + 1):
                total = total + gram_row(i)
        else:
            to_native(k)
            write_out(k)
            total = total + gram_row(n_prev + k)
    for c in range(comps):
        finish_round(n_steps, c)
        absorb(n_steps, c)

    to_native(n_steps)
    total = total + gram_row(n_vec - 1)
    gram_send[...] = total

    def scatter(slot, device):
        pltpu.make_async_remote_copy(
            src_ref=gram_send,
            dst_ref=gram_recv.at[slot],
            send_sem=gram_sems.at[0],
            recv_sem=gram_sems.at[1],
            device_id=device,
            device_id_type=MESH,
        ).start()

    each_other(scatter)
    write_out(n_steps)
    for step in range(n_steps + 1):
        for c in range(comps):
            for d in dirs_of(step):

                @pl.when(inside(*d))
                def _(c=c, d=d, step=step):
                    copy_of(step, c, d).wait_send()

    for i in range(2):
        pltpu.make_async_copy(gram_recv, gram_recv, gram_sems.at[i]).wait()
    full = (total + jnp.sum(gram_recv[...], axis=0)) * (1.0 / (rows * 2 * half_y * n_dev))
    for i in range(n_vec):
        line = full if i == 0 else pltpu.roll(full, half_y - i * n_vec, 1)
        gram_ref[i : i + 1, :] = line[:, :n_vec]


def on_device(residual, prev_basis, layer_ids, viscosity, shifts):
    n_lat = lax.axis_size("lat")
    n_rad = lax.axis_size("rad")
    comps, node_r, node_x, node_y = residual.shape
    n_prev = prev_basis.shape[0]
    n_steps = shifts.shape[0]
    n_vec = n_prev + n_steps + 1
    rows = comps * node_r * node_x
    half_y = node_y // 2
    assert node_r == 8 and node_x == 8 and half_y == 128
    rounds = n_steps + 1
    tile = (8, half_y)
    vmem = pltpu.VMEM
    hbm_spec = pl.BlockSpec(memory_space=pltpu.HBM)
    vmem_spec = pl.BlockSpec(memory_space=pltpu.VMEM)
    out, gram = pl.pallas_call(
        functools.partial(kernel, n_lat, n_rad, n_steps, n_prev, comps),
        out_shape=(
            pltpu.VMEM((n_steps, rows, node_y), F32),
            pltpu.VMEM((n_vec, n_vec), F32),
        ),
        in_specs=[hbm_spec] * 5,
        out_specs=(vmem_spec, vmem_spec),
        scratch_shapes=[
            vmem((n_prev + 1, rows, node_y), F32),
            vmem(layer_ids.shape, jnp.int32),
            pltpu.SMEM(viscosity.shape, F32),
            pltpu.SMEM(shifts.shape, F32),
            vmem((n_vec, 2, rows, half_y), F32),
            vmem((2, comps, 4, 2, 2) + tile, F32),
            vmem((2, comps, 2, 2) + tile, F32),
            vmem((2, comps, 4, 2) + tile, F32),
            vmem((2, comps, 2) + tile, F32),
            vmem((2, 9) + tile, F32),
            vmem((rounds, comps, 2, 18, half_y), F32),
            vmem((rounds, comps, 2, 18, half_y), F32),
            vmem((rounds, comps, 4, 2, half_y), F32),
            vmem((rounds, comps, 2, 18, half_y), F32),
            vmem((rounds, comps, 2, 18, half_y), F32),
            vmem((rounds, comps, 4, 2, half_y), F32),
            vmem((1, half_y), F32),
            vmem((n_lat * n_rad - 1, 1, half_y), F32),
            pltpu.SemaphoreType.DMA((5,)),
            pltpu.SemaphoreType.DMA((rounds, comps, 8)),
            pltpu.SemaphoreType.DMA((rounds, comps, 8)),
            pltpu.SemaphoreType.DMA((2,)),
        ],
        compiler_params=pltpu.CompilerParams(
            collective_id=0, has_side_effects=True, vmem_limit_bytes=65000000
        ),
    )(
        residual.reshape(rows, node_y),
        prev_basis.reshape(n_prev, rows, node_y),
        layer_ids,
        viscosity,
        shifts,
    )
    return out.reshape((n_steps,) + residual.shape), gram


def solution(mesh):
    placed = (
        P(None, "rad", "lat", None),
        P(None, None, "rad", "lat", None),
        P("rad", "lat", None),
        P(),
        P(),
    )
    return jax.shard_map(
        on_device,
        mesh=mesh,
        in_specs=placed,
        out_specs=(P(None, None, "rad", "lat", None), P()),
        check_vma=False,
    )
```

profile of v0, /device:TPU:0, one launch (start us, length us, event | category | flops | bytes accessed | tf_op | source)
XLA Modules:
  0.0 31.3 jit_solution(6864086514270209640)
XLA Ops:
  0.6 29.2 %shard_map.68 = (f32[4,192,256]{2,1,0:T(8,128)S(1)}, f32[9,9]{1,0:T(8,128)S(1)}) custom-call(f32[192,256]{1,0:T(8,128)} %bitcast.5, f32[4,192,256]{2,1,0:T(8,128)} %bitcast.4, s32[4,4,128]{2,1,0:T(4,128)} %ids_hbm.1, f32[8]{0:T(128)} %visc_hbm.1, f32[4]{0:T(128)} %shift_hbm.1), custom_call_target="tpu_custom_call" | custom-call | tf_op jit(solution)/shard_map/pallas_call | solution.py:512
  29.9 0.9 %copy.9 = f32[4,3,8,8,256]{4,3,2,1,0:T(8,128)} copy(f32[4,3,8,8,256]{4,3,2,1,0:T(8,128)S(1)} %bitcast.3) | data formatting | bytes 1572864
  30.7 0.6 %copy.10 = f32[9,9]{1,0:T(8,128)} copy(f32[9,9]{1,0:T(8,128)S(1)} %get-tuple-element.7) | data formatting | bytes 648
where the time goes:
time: 31.5 us; the launch traced here: 31.3 us
  Pallas kernels  29.2 us (93%)
  local copies, waits for them, and re-layouts  1.48 us (5%)
  between operations  0.64 us (2%)
    pallas_call x1, Pallas kernels, on_device(): pl.pallas_call(functools.partial(kernel, n_lat, n_rad, n_steps, n_prev, c...  29.2 us
    unnamed x2, local copies, waits for them, and re-layouts  1.48 us

commit v1 on v0

--- a/solution.py
+++ b/solution.py
@@ -14,7 +14,6 @@
 stiff = (0.0, 1.0, 4.0 / 3)
 
 DIRS = ((-1, -1), (-1, 0), (-1, 1), (0, -1), (0, 1), (1, -1), (1, 0), (1, 1))
-SLOT = {d: i for i, d in enumerate(DIRS)}
 R_DIRS = {(-1, 0): 0, (1, 0): 1}
 X_DIRS = {(0, -1): 0, (0, 1): 1}
 C_DIRS = {(-1, -1): 0, (-1, 1): 1, (1, -1): 2, (1, 1): 3}
@@ -71,10 +70,12 @@
     recv_c,
     gram_send,
     gram_recv,
+    bulk,
     in_sem,
     send_sem,
     recv_sem,
     gram_sems,
+    token_sem,
 ):
     n_dev = n_lat * n_rad
     lat = lax.axis_index("lat")
@@ -97,29 +98,76 @@
         copy.start()
     prev_copy.start()
 
-    recv_r[...] = jnp.zeros_like(recv_r)
-    recv_x[...] = jnp.zeros_like(recv_x)
-    recv_c[...] = jnp.zeros_like(recv_c)
-
     barrier = pltpu.get_barrier_semaphore()
 
+    def spread(pos, count, far):
+        return jnp.where(pos >= far, 1, 0) + jnp.where(pos < count - far, 1, 0)
+
+    def around(far):
+        return (1 + spread(rad, n_rad, far)) * (1 + spread(lat, n_lat, far)) - 1
+
+    def within(dr, dx):
+        ok = None
+        for pos, step, count in ((rad, dr, n_rad), (lat, dx, n_lat)):
+            if step:
+                one = (pos >= -step) if step < 0 else (pos < count - step)
+                ok = one if ok is None else jnp.logical_and(ok, one)
+        return ok
+
+    def signal_around(sem, far):
+        for dr, dx in DIRS:
+            if (dr and n_rad <= far) or (dx and n_lat <= far):
+                continue
+
+            @pl.when(within(dr * far, dx * far))
+            def _(dr=dr, dx=dx):
+                pl.semaphore_signal(
+                    sem,
+                    inc=1,
+                    device_id={"lat": lat + dx * far, "rad": rad + dr * far},
+                    device_id_type=MESH,
+                )
+
+    signal_around(barrier, 1)
+
+    for d in DIRS:
+        if d in R_DIRS:
+            ref, slot = recv_r, R_DIRS[d]
+        elif d in X_DIRS:
+            ref, slot = recv_x, X_DIRS[d]
+        else:
+            ref, slot = recv_c, C_DIRS[d]
+
+        @pl.when(jnp.logical_not(within(-d[0], -d[1])))
+        def _(ref=ref, slot=slot):
+            ref[:, :, slot] = jnp.zeros(ref.shape[:2] + ref.shape[3:], F32)
+
+    reaches = []
+    while (1 << len(reaches)) < max(n_lat, n_rad) - 1:
+        reaches.append(1 << len(reaches))
+
+    def send_token(j):
+        if j < len(reaches):
+            signal_around(token_sem.at[j], reaches[j])
+
+    def take_token(j):
+        if j < len(reaches):
+            pl.semaphore_wait(token_sem.at[j], around(reaches[j]))
+
     rad_targets = [lax.rem(rad + d, n_rad) for d in range(n_rad)]
 
     def each_other(visit):
-        def row(ahead, carry):
-            lat_target = lax.rem(lat + ahead, n_lat)
+        def row(i, carry):
+            lat_target = lax.rem(lat + n_lat // 2 + i, n_lat)
             for d in range(n_rad):
+                ahead = lax.rem(n_lat // 2 + i, n_lat)
                 visit(ahead * n_rad + d - 1, {"lat": lat_target, "rad": rad_targets[d]})
             return carry
 
-        lax.fori_loop(1, n_lat, row, 0, unroll=n_lat <= 8)
+        lax.fori_loop(0, n_lat // 2, row, 0, unroll=n_lat <= 8)
+        lax.fori_loop(n_lat // 2 + 1, n_lat, row, 0, unroll=n_lat <= 8)
         for d in range(1, n_rad):
             visit(d - 1, {"lat": lat, "rad": rad_targets[d]})
-
-    def greet(slot, device):
-        pl.semaphore_signal(barrier, inc=1, device_id=device, device_id_type=MESH)
-
-    each_other(greet)
 
     sub = lax.broadcasted_iota(jnp.int32, (8, half_y), 0)
     lane = lax.broadcasted_iota(jnp.int32, (8, half_y), 1)
@@ -147,13 +195,18 @@
     dst = lax.broadcasted_iota(jnp.int32, (2 * half_y, 2 * half_y), 1)
     split_perm = jnp.where(
         src == jnp.where(dst < half_y, 2 * dst, 2 * (dst - half_y) + 1), 1.0, 0.0
-    ).astype(F32)
+    ).astype(jnp.bfloat16)
     join_perm = jnp.where(
         dst == jnp.where(src < half_y, 2 * src, 2 * (src - half_y) + 1), 1.0, 0.0
-    ).astype(F32)
+    ).astype(jnp.bfloat16)
 
     def exact_dot(a, b):
-        return jnp.dot(a, b, precision=lax.Precision.HIGHEST, preferred_element_type=F32)
+        high = a.astype(jnp.bfloat16)
+        rest = a - high.astype(F32)
+        mid = rest.astype(jnp.bfloat16)
+        low = (rest - mid.astype(F32)).astype(jnp.bfloat16)
+        out = [jnp.dot(part, b, preferred_element_type=F32) for part in (high, mid, low)]
+        return out[0] + (out[1] + out[2])
 
     def split_columns(i):
         z = exact_dot(stage[i], split_perm)
@@ -180,20 +233,12 @@
         return pltpu.make_async_remote_copy(
             src_ref=a,
             dst_ref=b,
-            send_sem=send_sem.at[step, c, SLOT[d]],
-            recv_sem=recv_sem.at[step, c, SLOT[d]],
+            send_sem=send_sem.at[0],
+            recv_sem=recv_sem.at[step % 2, c],
             device_id={"lat": lat + d[1], "rad": rad + d[0]},
             device_id_type=MESH,
         )
 
-    def inside(dr, dx):
-        ok = None
-        for pos, step, count in ((rad, dr, n_rad), (lat, dx, n_lat)):
-            if step:
-                one = (pos > 0) if step < 0 else (pos < count - 1)
-                ok = one if ok is None else jnp.logical_and(ok, one)
-        return ok
-
     order = ((-1, -1), (1, 1), (-1, 1), (1, -1), (1, 0), (-1, 0), (0, 1), (0, -1))
 
     def dirs_of(step):
@@ -203,16 +248,41 @@
     def start_round(step, c):
         for d in dirs_of(step):
 
-            @pl.when(inside(*d))
+            @pl.when(within(*d))
             def _(d=d):
                 copy_of(step, c, d).start()
 
+    def places(pos, count):
+        out = [(pos == 0, False, True), (pos == count - 1, True, False)]
+        if count > 2:
+            middle = jnp.logical_and(pos > 0, pos < count - 1)
+            out.append((middle, True, True))
+        return out if count > 1 else [(pos == 0, False, False)]
+
+    def rows_of(dirs, down, up, left, right):
+        have = {-1: {0: True, -1: down, 1: up}, 1: {0: True, -1: left, 1: right}}
+        total = 0
+        for dr, dx in dirs:
+            if have[-1][dr] and have[1][dx]:
+                total += 2 if dr and dx else 18
+        return total
+
+    def settle(sem, dir_lists):
+        groups = {}
+        for at_r, down, up in places(rad, n_rad):
+            for at_x, left, right in places(lat, n_lat):
+                n = sum(rows_of(dirs, down, up, left, right) for dirs in dir_lists)
+                here = jnp.logical_and(at_r, at_x)
+                groups[n] = jnp.logical_or(groups[n], here) if n in groups else here
+        for n, here in groups.items():
+            if n:
+
+                @pl.when(here)
+                def _(n=n):
+                    pltpu.make_async_copy(bulk.at[pl.ds(0, n)], bulk.at[pl.ds(0, n)], sem).wait()
+
     def finish_round(step, c):
-        for d in dirs_of(step):
-
-            @pl.when(inside(-d[0], -d[1]))
-            def _(d=d):
-                copy_of(step, c, d).wait_recv()
+        settle(recv_sem.at[step % 2, c], [[(-d[0], -d[1]) for d in dirs_of(step)]])
 
     def pack_x(vals, at):
         out = None
@@ -370,15 +440,14 @@
                         edge = edge + ghost_x[new, c, ro, q]
                     ghost_x[new, c, ro, q] = edge * right_f
 
-    def to_native(k):
+    def to_native(k, c):
         cur = k % 2
-        for c in range(comps):
-            for ro in range(4):
-                for p in range(2):
-                    for q in range(2):
-                        v = vec[cur, c, ro, p, q]
-                        for h in range(2):
-                            work[n_prev + k, q, native(c, ro, p, h), :] = v[4 * h : 4 * h + 4]
+        for ro in range(4):
+            for p in range(2):
+                for q in range(2):
+                    v = vec[cur, c, ro, p, q]
+                    for h in range(2):
+                        work[n_prev + k, q, native(c, ro, p, h), :] = v[4 * h : 4 * h + 4]
 
     def write_out(k):
         z = jnp.concatenate([work[n_prev + k, 0], work[n_prev + k, 1]], 1)
@@ -387,7 +456,7 @@
     lane16 = lax.broadcasted_iota(jnp.int32, (16, half_y), 1)
     row16 = lax.broadcasted_iota(jnp.int32, (16, half_y), 0)
 
-    def gram_row(i):
+    def gram_part(i, acc, first, count):
         def chunk(t, acc):
             at = pl.ds(pl.multiple_of(8 * t, 8), 8)
             for q in range(2):
@@ -397,15 +466,21 @@
                 )
             return acc
 
-        acc = lax.fori_loop(
-            0, rows // 8, chunk, (jnp.zeros((8, half_y), F32),) * (i + 1), unroll=4
-        )
+        return lax.fori_loop(first, first + count, chunk, acc, unroll=4)
+
+    def gram_zero(i):
+        return (jnp.zeros((8, half_y), F32),) * (i + 1)
+
+    def gram_close(i, acc):
         sums = [jnp.sum(a, axis=0, keepdims=True) for a in acc]
         sums.append(jnp.zeros((16 - len(sums), half_y), F32))
         total = jnp.sum(jnp.concatenate(sums, 0), axis=1, keepdims=True)
         hit = jnp.logical_or(lane16 == i * n_vec + row16, lane16 == row16 * n_vec + i)
         hit = jnp.logical_and(hit, row16 <= i)
         return jnp.sum(jnp.where(hit, jnp.broadcast_to(total, hit.shape), 0.0), 0, keepdims=True)
+
+    def gram_row(i):
+        return gram_close(i, gram_part(i, gram_zero(i), 0, rows // 8))
 
     res_copy.wait()
     split_columns(n_prev)
@@ -428,9 +503,10 @@
             send_x[0, c, 0, face] = pack_x([vec[0, c, ro, 0, q] for ro in range(4)], 0)
             send_c[0, c, 0, q : q + 1] = vec[0, c, 0, 0, q, 0:1]
 
-    pl.semaphore_wait(barrier, n_dev - 1)
+    pl.semaphore_wait(barrier, around(1))
     for c in range(comps):
         start_round(0, c)
+    send_token(0)
     for copy in small_copies:
         copy.wait()
     for e in range(2):
@@ -451,19 +527,27 @@
             absorb(k, c)
             apply(k, c)
             start_round(k + 1, c)
+        take_token(k)
+        send_token(k + 1)
         if k == 0:
             for i in range(n_prev + 1):
                 total = total + gram_row(i)
         else:
-            to_native(k)
+            for c in range(comps):
+                to_native(k, c)
             write_out(k)
             total = total + gram_row(n_prev + k)
+    for j in range(n_steps, len(reaches)):
+        take_token(j)
+        send_token(j + 1)
+    acc = gram_zero(n_vec - 1)
+    per = rows // 8 // comps
     for c in range(comps):
         finish_round(n_steps, c)
         absorb(n_steps, c)
-
-    to_native(n_steps)
-    total = total + gram_row(n_vec - 1)
+        to_native(n_steps, c)
+        acc = gram_part(n_vec - 1, acc, c * per, per)
+    total = total + gram_close(n_vec - 1, acc)
     gram_send[...] = total
 
     def scatter(slot, device):
@@ -478,14 +562,7 @@
 
     each_other(scatter)
     write_out(n_steps)
-    for step in range(n_steps + 1):
-        for c in range(comps):
-            for d in dirs_of(step):
-
-                @pl.when(inside(*d))
-                def _(c=c, d=d, step=step):
-                    copy_of(step, c, d).wait_send()
-
+    settle(send_sem.at[0], [dirs_of(step) for step in range(n_steps + 1)] * comps)
     for i in range(2):
         pltpu.make_async_copy(gram_recv, gram_recv, gram_sems.at[i]).wait()
     full = (total + jnp.sum(gram_recv[...], axis=0)) * (1.0 / (rows * 2 * half_y * n_dev))
@@ -536,10 +613,12 @@
             vmem((rounds, comps, 4, 2, half_y), F32),
             vmem((1, half_y), F32),
             vmem((n_lat * n_rad - 1, 1, half_y), F32),
+            vmem((rounds * comps * 80, half_y), F32),
             pltpu.SemaphoreType.DMA((5,)),
-            pltpu.SemaphoreType.DMA((rounds, comps, 8)),
-            pltpu.SemaphoreType.DMA((rounds, comps, 8)),
+            pltpu.SemaphoreType.DMA((1,)),
+            pltpu.SemaphoreType.DMA((2, comps)),
             pltpu.SemaphoreType.DMA((2,)),
+            pltpu.SemaphoreType.REGULAR((max(n_lat, n_rad).bit_length(),)),
         ],
         compiler_params=pltpu.CompilerParams(
             collective_id=0, has_side_effects=True, vmem_limit_bytes=65000000

time: 31.5 us -> 29 us (0.921)
  Pallas kernels: 29.2 us -> 26.7 us
    pallas_call x1, Pallas kernels: 29.2 us -> 26.7 us  [on_device(): pl.pallas_call(functools.partial(kernel, n_lat, n_rad, n_steps, n_prev, c...]
where the time goes in v1:
time: 29 us; the launch traced here: 28.8 us
  Pallas kernels  26.7 us (92%)
  local copies, waits for them, and re-layouts  1.48 us (5%)
  between operations  0.64 us (2%)
    pallas_call x1, Pallas kernels, on_device(): pl.pallas_call(functools.partial(kernel, n_lat, n_rad, n_steps, n_prev, c...  26.7 us
    unnamed x2, local copies, waits for them, and re-layouts  1.48 us

profile of v1, /device:TPU:0, one launch (start us, length us, event | category | flops | bytes accessed | tf_op | source)
XLA Modules:
  0.0 28.8 jit_solution(4245033358348915967)
XLA Ops:
  0.6 26.7 %shard_map.68 = (f32[4,192,256]{2,1,0:T(8,128)S(1)}, f32[9,9]{1,0:T(8,128)S(1)}) custom-call(f32[192,256]{1,0:T(8,128)} %bitcast.5, f32[4,192,256]{2,1,0:T(8,128)} %bitcast.4, s32[4,4,128]{2,1,0:T(4,128)} %ids_hbm.1, f32[8]{0:T(128)} %visc_hbm.1, f32[4]{0:T(128)} %shift_hbm.1), custom_call_target="tpu_custom_call" | custom-call | tf_op jit(solution)/shard_map/pallas_call | solution.py:589
  27.3 0.9 %copy.9 = f32[4,3,8,8,256]{4,3,2,1,0:T(8,128)} copy(f32[4,3,8,8,256]{4,3,2,1,0:T(8,128)S(1)} %bitcast.3) | data formatting | bytes 1572864
  28.2 0.6 %copy.10 = f32[9,9]{1,0:T(8,128)} copy(f32[9,9]{1,0:T(8,128)S(1)} %get-tuple-element.7) | data formatting | bytes 648

commit v2 on v1

--- a/solution.py
+++ b/solution.py
@@ -571,6 +571,17 @@
         gram_ref[i : i + 1, :] = line[:, :n_vec]
 
 
+def store(vec_ref, gram_ref, vec_out, gram_out, sems):
+    copies = [
+        pltpu.make_async_copy(vec_ref, vec_out, sems.at[0]),
+        pltpu.make_async_copy(gram_ref, gram_out, sems.at[1]),
+    ]
+    for copy in copies:
+        copy.start()
+    for copy in copies:
+        copy.wait()
+
+
 def on_device(residual, prev_basis, layer_ids, viscosity, shifts):
     n_lat = lax.axis_size("lat")
     n_rad = lax.axis_size("rad")
@@ -630,6 +641,16 @@
         viscosity,
         shifts,
     )
+    out, gram = pl.pallas_call(
+        store,
+        out_shape=(
+            jax.ShapeDtypeStruct(out.shape, F32),
+            jax.ShapeDtypeStruct(gram.shape, F32),
+        ),
+        in_specs=[vmem_spec] * 2,
+        out_specs=(hbm_spec, hbm_spec),
+        scratch_shapes=[pltpu.SemaphoreType.DMA((2,))],
+    )(*(pltpu.with_memory_space_constraint(a, pltpu.VMEM) for a in (out, gram)))
     return out.reshape((n_steps,) + residual.shape), gram
 
 

time: 29 us -> 28.4 us (0.979)
  local copies, waits for them, and re-layouts: 1.48 us -> 0 us
  Pallas kernels: 26.7 us -> 27.6 us
    unnamed x2 -> x0, local copies, waits for them, and re-layouts: 1.48 us -> none
    pallas_call x0 -> x1, Pallas kernels: none -> 0.9 us  [on_device(): pl.pallas_call(store, out_shape=(jax.ShapeDtypeStruct(out.shape, F32), ja...]
where the time goes in v2:
time: 28.4 us; the launch traced here: 28.3 us
  Pallas kernels  27.6 us (97%)
  between operations  0.64 us (2%)
    pallas_call x1, Pallas kernels, on_device(): pl.pallas_call(functools.partial(kernel, n_lat, n_rad, n_steps, n_prev, c...  26.7 us
    pallas_call x1, Pallas kernels, on_device(): pl.pallas_call(store, out_shape=(jax.ShapeDtypeStruct(out.shape, F32), ja...  0.9 us

profile of v2, /device:TPU:0, one launch (start us, length us, event | category | flops | bytes accessed | tf_op | source)
XLA Modules:
  0.0 28.3 jit_solution(7500626281423933723)
XLA Ops:
  0.6 26.7 %shard_map.68 = (f32[4,192,256]{2,1,0:T(8,128)S(1)}, f32[9,9]{1,0:T(8,128)S(1)}) custom-call(f32[192,256]{1,0:T(8,128)} %bitcast.4, f32[4,192,256]{2,1,0:T(8,128)} %bitcast.3, s32[4,4,128]{2,1,0:T(4,128)} %ids_hbm.1, f32[8]{0:T(128)} %visc_hbm.1, f32[4]{0:T(128)} %shift_hbm.1), custom_call_target="tpu_custom_call" | custom-call | tf_op jit(solution)/shard_map/pallas_call | solution.py:600
  27.3 0.9 %shard_map.69 = (f32[4,192,256]{2,1,0:T(8,128)}, f32[9,9]{1,0:T(8,128)}) custom-call(f32[4,192,256]{2,1,0:T(8,128)S(1)} %get-tuple-element.6.vec_ref, f32[9,9]{1,0:T(8,128)S(1)} %get-tuple-element.7.gram_ref), custom_call_target="tpu_custom_call" | custom-call | tf_op jit(solution)/shard_map/pallas_call | solution.py:644

commit v3 on v2

--- a/solution.py
+++ b/solution.py
@@ -100,11 +100,12 @@
 
     barrier = pltpu.get_barrier_semaphore()
 
-    def spread(pos, count, far):
-        return jnp.where(pos >= far, 1, 0) + jnp.where(pos < count - far, 1, 0)
-
-    def around(far):
-        return (1 + spread(rad, n_rad, far)) * (1 + spread(lat, n_lat, far)) - 1
+    def around(far, dirs):
+        total = 0
+        for dr, dx in dirs:
+            if not ((dr and n_rad <= far) or (dx and n_lat <= far)):
+                total += jnp.where(within(dr * far, dx * far), 1, 0)
+        return total
 
     def within(dr, dx):
         ok = None
@@ -114,8 +115,8 @@
                 ok = one if ok is None else jnp.logical_and(ok, one)
         return ok
 
-    def signal_around(sem, far):
-        for dr, dx in DIRS:
+    def signal_around(sem, far, dirs):
+        for dr, dx in dirs:
             if (dr and n_rad <= far) or (dx and n_lat <= far):
                 continue
 
@@ -128,7 +129,7 @@
                     device_id_type=MESH,
                 )
 
-    signal_around(barrier, 1)
+    signal_around(barrier, 1, LAST)
 
     for d in DIRS:
         if d in R_DIRS:
@@ -143,16 +144,16 @@
             ref[:, :, slot] = jnp.zeros(ref.shape[:2] + ref.shape[3:], F32)
 
     reaches = []
-    while (1 << len(reaches)) < max(n_lat, n_rad) - 1:
-        reaches.append(1 << len(reaches))
+    while (2 << len(reaches)) < max(n_lat, n_rad) - 1:
+        reaches.append(2 << len(reaches))
 
     def send_token(j):
         if j < len(reaches):
-            signal_around(token_sem.at[j], reaches[j])
+            signal_around(token_sem.at[j], reaches[j], DIRS)
 
     def take_token(j):
         if j < len(reaches):
-            pl.semaphore_wait(token_sem.at[j], around(reaches[j]))
+            pl.semaphore_wait(token_sem.at[j], around(reaches[j], DIRS))
 
     rad_targets = [lax.rem(rad + d, n_rad) for d in range(n_rad)]
 
@@ -483,6 +484,28 @@
         return gram_close(i, gram_part(i, gram_zero(i), 0, rows // 8))
 
     res_copy.wait()
+    edge_rows = []
+    for c in range(comps):
+        picked = [2 * x + p for p in range(2) for x in range(4)] + [8 * r for r in range(8)]
+        edge_rows += [stage[n_prev, pl.ds(c * 64 + at, 1), :] for at in picked]
+    edge = exact_dot(jnp.concatenate(edge_rows, 0), split_perm)
+    zero_rows = jnp.zeros((2, half_y), F32)
+    for c in range(comps):
+        send_r[0, c, 0, 16:18] = zero_rows
+        send_x[0, c, 0, 16:18] = zero_rows
+        for q in range(2):
+            face = slice(8 * q, 8 * q + 8)
+            lanes = slice(half_y * q, half_y * (q + 1))
+            send_r[0, c, 0, face] = edge[16 * c : 16 * c + 8, lanes]
+            send_x[0, c, 0, face] = edge[16 * c + 8 : 16 * c + 16, lanes]
+            send_c[0, c, 0, q : q + 1] = edge[16 * c : 16 * c + 1, lanes]
+
+    @pl.when(jnp.logical_or(rad > 0, lat > 0))
+    def _():
+        pl.semaphore_wait(barrier, around(1, FIRST))
+
+    for c in range(comps):
+        start_round(0, c)
     split_columns(n_prev)
     for c in range(comps):
         for ro in range(4):
@@ -491,22 +514,6 @@
                     vec[0, c, ro, p, q] = jnp.concatenate(
                         [work[n_prev, q, native(c, ro, p, h), :] for h in range(2)], 0
                     )
-    zero_rows = jnp.zeros((2, half_y), F32)
-    for c in range(comps):
-        send_r[0, c, 0, 16:18] = zero_rows
-        send_x[0, c, 0, 16:18] = zero_rows
-        for q in range(2):
-            face = slice(8 * q, 8 * q + 8)
-            send_r[0, c, 0, face] = jnp.where(
-                upper, roll_s(vec[0, c, 0, 1, q], 4), vec[0, c, 0, 0, q]
-            )
-            send_x[0, c, 0, face] = pack_x([vec[0, c, ro, 0, q] for ro in range(4)], 0)
-            send_c[0, c, 0, q : q + 1] = vec[0, c, 0, 0, q, 0:1]
-
-    pl.semaphore_wait(barrier, around(1))
-    for c in range(comps):
-        start_round(0, c)
-    send_token(0)
     for copy in small_copies:
         copy.wait()
     for e in range(2):
@@ -527,8 +534,10 @@
             absorb(k, c)
             apply(k, c)
             start_round(k + 1, c)
-        take_token(k)
-        send_token(k + 1)
+        if k >= 2:
+            take_token(k - 2)
+        if k >= 1:
+            send_token(k - 1)
         if k == 0:
             for i in range(n_prev + 1):
                 total = total + gram_row(i)
@@ -537,7 +546,8 @@
                 to_native(k, c)
             write_out(k)
             total = total + gram_row(n_prev + k)
-    for j in range(n_steps, len(reaches)):
+    assert n_steps >= 2
+    for j in range(n_steps - 2, len(reaches)):
         take_token(j)
         send_token(j + 1)
     acc = gram_zero(n_vec - 1)

time: 28.4 us -> 28.3 us (level)
  no operation moved by 1% of the time
where the time goes in v3:
time: 28.3 us; the launch traced here: 28.2 us
  Pallas kernels  27.5 us (97%)
  between operations  0.64 us (2%)
    pallas_call x1, Pallas kernels, on_device(): pl.pallas_call(functools.partial(kernel, n_lat, n_rad, n_steps, n_prev, c...  26.6 us
    pallas_call x1, Pallas kernels, on_device(): pl.pallas_call(store, out_shape=(jax.ShapeDtypeStruct(out.shape, F32), ja...  0.9 us

profile of v3, /device:TPU:0, one launch (start us, length us, event | category | flops | bytes accessed | tf_op | source)
XLA Modules:
  0.0 28.2 jit_solution(9495706325322673235)
XLA Ops:
  0.6 26.6 %shard_map.68 = (f32[4,192,256]{2,1,0:T(8,128)S(1)}, f32[9,9]{1,0:T(8,128)S(1)}) custom-call(f32[192,256]{1,0:T(8,128)} %bitcast.4, f32[4,192,256]{2,1,0:T(8,128)} %bitcast.3, s32[4,4,128]{2,1,0:T(4,128)} %ids_hbm.1, f32[8]{0:T(128)} %visc_hbm.1, f32[4]{0:T(128)} %shift_hbm.1), custom_call_target="tpu_custom_call" | custom-call | tf_op jit(solution)/shard_map/pallas_call | solution.py:610
  27.3 0.9 %shard_map.69 = (f32[4,192,256]{2,1,0:T(8,128)}, f32[9,9]{1,0:T(8,128)}) custom-call(f32[4,192,256]{2,1,0:T(8,128)S(1)} %get-tuple-element.6.vec_ref, f32[9,9]{1,0:T(8,128)S(1)} %get-tuple-element.7.gram_ref), custom_call_target="tpu_custom_call" | custom-call | tf_op jit(solution)/shard_map/pallas_call | solution.py:654

commit v4 on v3

--- a/solution.py
+++ b/solution.py
@@ -19,6 +19,17 @@
 C_DIRS = {(-1, -1): 0, (-1, 1): 1, (1, -1): 2, (1, 1): 3}
 FIRST = ((-1, 0), (0, -1), (-1, -1))
 LAST = ((1, 0), (0, 1), (1, 1))
+ROWS_X, ROWS_G, ROWS_A, ROWS_C = 0, 8, 12, 16
+RIM = (
+    ((1, 0), (0, 8), (4, 4), ROWS_X, 0),
+    ((1, 0), (16, 4), (7, 1), ROWS_G, 3),
+    ((0, 1), (8, 8), (4, 4), ROWS_X, 4),
+    ((0, 1), (20, 4), (7, 1), ROWS_G, 7),
+    ((1, 1), (24, 4), (7, 1), ROWS_C, 0),
+    ((1, 1), (28, 4), (7, 1), ROWS_C, 4),
+    ((1, -1), (32, 4), (4, 1), ROWS_A, 3),
+    ((-1, 1), (36, 4), (3, 1), ROWS_A, 7),
+)
 
 
 def weight(a, b, c):
@@ -71,9 +82,18 @@
     gram_send,
     gram_recv,
     bulk,
+    rim_send,
+    rim_recv,
+    block_send,
+    block_recv,
+    eta_send,
+    eta_recv,
+    rim_scaled,
+    rim_own,
     in_sem,
     send_sem,
     recv_sem,
+    rim_sems,
     gram_sems,
     token_sem,
 ):
@@ -142,6 +162,9 @@
         @pl.when(jnp.logical_not(within(-d[0], -d[1])))
         def _(ref=ref, slot=slot):
             ref[:, :, slot] = jnp.zeros(ref.shape[:2] + ref.shape[3:], F32)
+
+    for ref in (rim_recv, block_recv, eta_recv):
+        ref[...] = jnp.zeros_like(ref)
 
     reaches = []
     while (2 << len(reaches)) < max(n_lat, n_rad) - 1:
@@ -243,7 +266,7 @@
     order = ((-1, -1), (1, 1), (-1, 1), (1, -1), (1, 0), (-1, 0), (0, 1), (0, -1))
 
     def dirs_of(step):
-        wanted = FIRST if step == 0 else (LAST if step == n_steps else DIRS)
+        wanted = FIRST if step == 0 else DIRS
         return [d for d in order if d in wanted]
 
     def start_round(step, c):
@@ -260,19 +283,15 @@
             out.append((middle, True, True))
         return out if count > 1 else [(pos == 0, False, False)]
 
-    def rows_of(dirs, down, up, left, right):
+    def rows_of(sizes, down, up, left, right):
         have = {-1: {0: True, -1: down, 1: up}, 1: {0: True, -1: left, 1: right}}
-        total = 0
-        for dr, dx in dirs:
-            if have[-1][dr] and have[1][dx]:
-                total += 2 if dr and dx else 18
-        return total
-
-    def settle(sem, dir_lists):
+        return sum(n for (dr, dx), n in sizes if have[-1][dr] and have[1][dx])
+
+    def settle(sem, sizes):
         groups = {}
         for at_r, down, up in places(rad, n_rad):
             for at_x, left, right in places(lat, n_lat):
-                n = sum(rows_of(dirs, down, up, left, right) for dirs in dir_lists)
+                n = rows_of(sizes, down, up, left, right)
                 here = jnp.logical_and(at_r, at_x)
                 groups[n] = jnp.logical_or(groups[n], here) if n in groups else here
         for n, here in groups.items():
@@ -282,8 +301,55 @@
                 def _(n=n):
                     pltpu.make_async_copy(bulk.at[pl.ds(0, n)], bulk.at[pl.ds(0, n)], sem).wait()
 
+    def opposite(sizes):
+        return [((-dr, -dx), n) for (dr, dx), n in sizes]
+
+    def round_sizes(step):
+        return [(d, 2 if d[0] and d[1] else 18) for d in dirs_of(step)]
+
+    rim_sizes = [(d, comps * count * high) for d, (_, count), (_, high), _, _ in RIM]
+    rim_sizes.append(((1, 1), comps * 8))
+    eta_sizes = [((1, 0), 4), ((0, 1), 4), ((1, 1), 1)]
+
     def finish_round(step, c):
-        settle(recv_sem.at[step % 2, c], [[(-d[0], -d[1]) for d in dirs_of(step)]])
+        settle(recv_sem.at[step % 2, c], opposite(round_sizes(step)))
+
+    def remote(a, b, recv, d):
+        @pl.when(within(*d))
+        def _():
+            pltpu.make_async_remote_copy(
+                src_ref=a,
+                dst_ref=b,
+                send_sem=send_sem.at[0],
+                recv_sem=recv,
+                device_id={"lat": lat + d[1], "rad": rad + d[0]},
+                device_id_type=MESH,
+            ).start()
+
+    def start_rim():
+        for d, (first, count), (row, high), to, to_row in RIM:
+            remote(
+                rim_send.at[:, pl.ds(first, count), pl.ds(row, high)],
+                rim_recv.at[:, pl.ds(to, count), pl.ds(to_row, high)],
+                rim_sems.at[0],
+                d,
+            )
+        remote(
+            block_send.at[:, pl.ds(0, comps)], block_recv.at[:, pl.ds(0, comps)], rim_sems.at[0], (1, 1)
+        )
+
+    def start_eta():
+        for d, slot, row, high, to, to_row in (
+            ((1, 0), 0, 4, 4, 0, 0),
+            ((0, 1), 1, 4, 4, 0, 4),
+            ((1, 1), 0, 7, 1, 1, 0),
+        ):
+            remote(
+                eta_send.at[slot, pl.ds(row, high)],
+                eta_recv.at[to, pl.ds(to_row, high)],
+                rim_sems.at[1],
+                d,
+            )
 
     def pack_x(vals, at):
         out = None
@@ -291,6 +357,24 @@
             moved = roll_s(vals[ro], ro - at)
             out = moved if out is None else jnp.where(ex == ro, moved, out)
         return out
+
+    def y_pass(x0, x1, a, b, scale):
+        nxt = keep(lane != half_y - 1, pltpu.roll(x0, half_y - 1, 1))
+        m = list(forward(x0, x1, nxt))
+        for j in range(3):
+            key = tuple(sorted((a, b, j)))
+            m[j] = m[j] * scale(kinds[key]) if key in kinds else None
+        if m[0] is None:
+            r0 = m[1] + m[2]
+            r1 = -(m[2] + m[2])
+            r2 = m[2] - m[1]
+        else:
+            r0, r1, r2 = backward(*m)
+        return r0 + keep(lane != 0, pltpu.roll(r2, 1, 1)), r1
+
+    def to_column(low, high):
+        moved = jnp.where(sub == 6, roll_s(low, -1), high)
+        return jnp.where(sub == 4, roll_s(low, 1), jnp.where(sub == 5, roll_s(high, 2), moved))
 
     def apply(k, c):
         s = shift_ref[k]
@@ -322,22 +406,7 @@
                 for q in range(2):
                     x[0, q], x[1, q], x[2, q] = forward(t[a, 0, q], t[a, 1, q], t[a, 2, q])
                 for b in range(3):
-                    nxt = keep(lane != half_y - 1, pltpu.roll(x[b, 0], half_y - 1, 1))
-                    m = list(forward(x[b, 0], x[b, 1], nxt))
-                    for j in range(3):
-                        key = tuple(sorted((a, b, j)))
-                        if key in kinds:
-                            m[j] = m[j] * scaled[e, kinds[key]]
-                        else:
-                            m[j] = None
-                    if m[0] is None:
-                        r0 = m[1] + m[2]
-                        r1 = -(m[2] + m[2])
-                        r2 = m[2] - m[1]
-                    else:
-                        r0, r1, r2 = backward(*m)
-                    x[b, 0] = r0 + keep(lane != 0, pltpu.roll(r2, 1, 1))
-                    x[b, 1] = r1
+                    x[b, 0], x[b, 1] = y_pass(x[b, 0], x[b, 1], a, b, lambda i: scaled[e, i])
                 for q in range(2):
                     w[a, 0, q], w[a, 1, q], w[a, 2, q] = backward(x[0, q], x[1, q], x[2, q])
             for p in range(3):
@@ -361,12 +430,12 @@
             face = slice(8 * q, 8 * q + 8)
             edge = slice(16 + q, 17 + q)
             row = slice(q, q + 1)
-            send_r[step, c, 1, face] = jnp.where(upper, res[4, 1, q], roll_s(res[4, 0, q], 4))
-            send_r[step, c, 1, edge] = px[4, q][7:8]
-            send_x[step, c, 1, face] = pack_x([px[ro, q] for ro in range(4)], 3)
-            send_x[step, c, 1, edge] = px[4, q][7:8]
-            send_c[step, c, 3, row] = px[4, q][7:8]
             if not last:
+                send_r[step, c, 1, face] = jnp.where(upper, res[4, 1, q], roll_s(res[4, 0, q], 4))
+                send_r[step, c, 1, edge] = px[4, q][7:8]
+                send_x[step, c, 1, face] = pack_x([px[ro, q] for ro in range(4)], 3)
+                send_x[step, c, 1, edge] = px[4, q][7:8]
+                send_c[step, c, 3, row] = px[4, q][7:8]
                 send_r[step, c, 0, face] = jnp.where(upper, roll_s(res[0, 1, q], 4), res[0, 0, q])
                 send_r[step, c, 0, edge] = px[0, q][3:4]
                 send_x[step, c, 0, face] = pack_x([res[ro, 0, q] for ro in range(4)], 0)
@@ -383,10 +452,112 @@
                 for p in range(2):
                     ghost_r[new, c, p, q] = res[4, p, q] - s * u[4, p, q]
                 ghost_c[new, c, q] = px[4, q] - s * gx[4, q]
+            if step == n_steps - 1:
+                for n in range(2):
+                    rim_send[c, 24 + 2 * n + q] = px[2 + n, q]
+                    rim_send[c, 28 + 2 * n + q] = res[4, n, q]
+                    rim_send[c, 32 + 2 * n + q] = res[2 + n, 0, q]
+                    rim_send[c, 36 + 2 * n + q] = res[0, n, q]
+
+    def pack_rim(c):
+        new = (n_steps - 1) % 2
+        for q in range(2):
+            for n in range(2):
+                for p in range(2):
+                    v = vec[new, c, 2 + n, p, q]
+                    rim_send[c, 4 * n + 2 * p + q] = v
+                    block_send[4 * n + 2 * p + q, c : c + 1] = v[7:8]
+                    rim_send[c, 8 + 4 * n + 2 * p + q] = to_column(
+                        vec[new, c, p, n, q], vec[new, c, 2 + p, n, q]
+                    )
+                rim_send[c, 16 + 2 * n + q] = ghost_x[new, c, 2 + n, q]
+                rim_send[c, 20 + 2 * n + q] = ghost_r[new, c, n, q]
+
+    group_last = lax.rem(sub, 4) == 3
+    group_first = lax.rem(sub, 4) == 0
+
+    def own_planes(c):
+        cur = (n_steps - 1) % 2
+        for q in range(2):
+            side = jnp.where(corner3, ghost_x[cur, c, 0, q], roll_s(ghost_r[cur, c, 0, q], 3))
+            for p in range(2):
+                column = to_column(
+                    roll_s(vec[cur, c, p, 0, q], 3), roll_s(vec[cur, c, 2 + p, 0, q], 3)
+                )
+                plane = jnp.where(upper, column, vec[cur, c, 0, p, q])
+                rim_own[c, 2 * p + q] = plane
+                if p == 0:
+                    rim_own[c, 4 + q] = jnp.where(group_last, side, roll_s(plane, -1))
+
+    def rim_elements(u, scale):
+        t = {}
+        for p in range(3):
+            for q in range(2):
+                t[0, p, q], t[1, p, q], t[2, p, q] = forward(u[0, p, q], u[1, p, q], u[2, p, q])
+        w = {}
+        for a in range(3):
+            x = {}
+            for q in range(2):
+                x[0, q], x[1, q], x[2, q] = forward(t[a, 0, q], t[a, 1, q], t[a, 2, q])
+            for b in range(3):
+                x[b, 0], x[b, 1] = y_pass(x[b, 0], x[b, 1], a, b, scale)
+            for q in range(2):
+                w[a, 0, q], w[a, 1, q], w[a, 2, q] = backward(x[0, q], x[1, q], x[2, q])
+        return {
+            (p, q): w[0, p, q] + w[2, p, q] - w[1, p, q] for p in range(3) for q in range(2)
+        }
+
+    def add_rim():
+        cur = (n_steps - 1) % 2
+        new = 1 - cur
+        inner = jnp.where(upper, up_f, right_f)
+        corner = {}
+        sides = {}
+        for c in range(comps):
+            u = {}
+            for q in range(2):
+                for n in range(2):
+                    for p in range(2):
+                        u[n, p, q] = rim_recv[c, ROWS_X + 4 * n + 2 * p + q]
+                    u[n, 0, q] = u[n, 0, q] + rim_recv[c, ROWS_C + 2 * n + q]
+                    ghost = rim_recv[c, ROWS_G + 2 * n + q] + rim_recv[c, ROWS_A + 2 * n + q]
+                    u[n, 2, q] = jnp.where(group_last, ghost * inner, roll_s(u[n, 0, q], -1))
+                for p in range(3):
+                    u[2, p, q] = rim_own[c, 2 * p + q]
+            for q in range(2):
+                parts = {(2, 2): roll_s(u[2, 0, q], c)}
+                for n in range(2):
+                    parts[n, 2] = roll_s(u[n, 0, q], c)
+                    parts[2, n] = roll_s(u[n, 0, q], c - 4)
+                for key, part in parts.items():
+                    part = keep(sub == c, part)
+                    key = key + (q,)
+                    corner[key] = corner[key] + part if c else part
+            sides[c] = rim_elements(u, lambda i: rim_scaled[0, i])
+        for q in range(2):
+            for n in range(2):
+                for p in range(2):
+                    corner[n, p, q] = block_recv[4 * n + 2 * p + q]
+        tip = rim_elements(corner, lambda i: rim_scaled[1, i])
+        for c in range(comps):
+            for q in range(2):
+                out = [
+                    sides[c][0, q] + keep(~group_first, roll_s(sides[c][2, q], 1)),
+                    sides[c][1, q],
+                ]
+                for p in range(2):
+                    for e in range(2):
+                        ro = 2 * e + p
+                        add = keep(corner4, roll_s(out[p], -(2 + e)))
+                        add = jnp.where(corner0, roll_s(out[p], -(4 + e)), add)
+                        if ro == 0:
+                            add = add + keep(~upper, out[0]) + keep(corner0, roll_s(tip[2, q], -c))
+                        vec[new, c, ro, 0, q] += add
+                vec[new, c, 0, 1, q] += keep(~upper, out[1])
 
     def absorb(step, c):
         new = step % 2
-        first, last = step == 0, step == n_steps
+        first, last = step == 0, False
         for q in range(2):
             face = slice(8 * q, 8 * q + 8)
             line = slice(16 + q, 17 + q)
@@ -441,10 +612,12 @@
                         edge = edge + ghost_x[new, c, ro, q]
                     ghost_x[new, c, ro, q] = edge * right_f
 
-    def to_native(k, c):
+    def to_native(k, c, rim=False):
         cur = k % 2
         for ro in range(4):
             for p in range(2):
+                if rim and ro and p:
+                    continue
                 for q in range(2):
                     v = vec[cur, c, ro, p, q]
                     for h in range(2):
@@ -468,6 +641,15 @@
             return acc
 
         return lax.fori_loop(first, first + count, chunk, acc, unroll=4)
+
+    def gram_add(i, acc, at, mask):
+        for q in range(2):
+            mine = work[i, q, at, :]
+            mine = mine if mask is None else keep(mask, mine)
+            acc = tuple(
+                acc[j] + mine * (mine if j == i else work[j, q, at, :]) for j in range(i + 1)
+            )
+        return acc
 
     def gram_zero(i):
         return (jnp.zeros((8, half_y), F32),) * (i + 1)
@@ -516,13 +698,17 @@
                     )
     for copy in small_copies:
         copy.wait()
+    etas = []
     for e in range(2):
         ids = jnp.concatenate([ids_ref[e], ids_ref[2 + e]], 0)
         eta = jnp.zeros((8, half_y), F32)
         for layer in range(visc_ref.shape[0]):
             eta = eta + jnp.where(ids == layer, visc_ref[layer], 0.0)
+        etas.append(eta)
         for key, i in kinds.items():
             scaled[e, i] = eta * weight(*key)
+    eta_send[0] = etas[1]
+    eta_send[1] = to_column(*etas)
     prev_copy.wait()
     for i in range(n_prev):
         split_columns(i)
@@ -533,7 +719,14 @@
             finish_round(k, c)
             absorb(k, c)
             apply(k, c)
-            start_round(k + 1, c)
+            if k + 1 < n_steps:
+                start_round(k + 1, c)
+        if k == 0:
+            start_eta()
+        if k == n_steps - 2:
+            for c in range(comps):
+                pack_rim(c)
+            start_rim()
         if k >= 2:
             take_token(k - 2)
         if k >= 1:
@@ -546,17 +739,37 @@
                 to_native(k, c)
             write_out(k)
             total = total + gram_row(n_prev + k)
+        if k == n_steps - 2:
+            settle(rim_sems.at[1], opposite(eta_sizes))
+            tip_eta = jnp.broadcast_to(eta_recv[1, 0:1], (8, half_y))
+            for key, i in kinds.items():
+                rim_scaled[0, i] = eta_recv[0] * weight(*key)
+                rim_scaled[1, i] = tip_eta * weight(*key)
     assert n_steps >= 2
     for j in range(n_steps - 2, len(reaches)):
         take_token(j)
         send_token(j + 1)
+    for c in range(comps):
+        own_planes(c)
+        to_native(n_steps, c)
     acc = gram_zero(n_vec - 1)
-    per = rows // 8 // comps
     for c in range(comps):
-        finish_round(n_steps, c)
-        absorb(n_steps, c)
-        to_native(n_steps, c)
-        acc = gram_part(n_vec - 1, acc, c * per, per)
+        acc = lax.fori_loop(
+            8 * c + 1,
+            8 * c + 8,
+            lambda t, acc: gram_add(
+                n_vec - 1, acc, pl.ds(pl.multiple_of(8 * t, 8), 8), jnp.logical_not(corner0)
+            ),
+            acc,
+            unroll=7,
+        )
+    settle(rim_sems.at[0], opposite(rim_sizes))
+    add_rim()
+    for c in range(comps):
+        to_native(n_steps, c, rim=True)
+    for c in range(comps):
+        acc = gram_add(n_vec - 1, acc, pl.ds(c * 64, 8), None)
+        acc = gram_add(n_vec - 1, acc, pl.ds(c * 64, 8, stride=8), jnp.logical_not(corner0))
     total = total + gram_close(n_vec - 1, acc)
     gram_send[...] = total
 
@@ -572,7 +785,8 @@
 
     each_other(scatter)
     write_out(n_steps)
-    settle(send_sem.at[0], [dirs_of(step) for step in range(n_steps + 1)] * comps)
+    sent = [size for step in range(n_steps) for size in round_sizes(step)] * comps
+    settle(send_sem.at[0], sent + rim_sizes + eta_sizes)
     for i in range(2):
         pltpu.make_async_copy(gram_recv, gram_recv, gram_sems.at[i]).wait()
     full = (total + jnp.sum(gram_recv[...], axis=0)) * (1.0 / (rows * 2 * half_y * n_dev))
@@ -602,7 +816,7 @@
     rows = comps * node_r * node_x
     half_y = node_y // 2
     assert node_r == 8 and node_x == 8 and half_y == 128
-    rounds = n_steps + 1
+    rounds = n_steps
     tile = (8, half_y)
     vmem = pltpu.VMEM
     hbm_spec = pl.BlockSpec(memory_space=pltpu.HBM)
@@ -634,10 +848,19 @@
             vmem((rounds, comps, 4, 2, half_y), F32),
             vmem((1, half_y), F32),
             vmem((n_lat * n_rad - 1, 1, half_y), F32),
-            vmem((rounds * comps * 80, half_y), F32),
+            vmem((rounds * comps * 80 + 128 * comps, half_y), F32),
+            vmem((comps, 40) + tile, F32),
+            vmem((comps, 20) + tile, F32),
+            vmem((8,) + tile, F32),
+            vmem((8,) + tile, F32),
+            vmem((2,) + tile, F32),
+            vmem((2,) + tile, F32),
+            vmem((2, 9) + tile, F32),
+            vmem((comps, 6) + tile, F32),
             pltpu.SemaphoreType.DMA((5,)),
             pltpu.SemaphoreType.DMA((1,)),
             pltpu.SemaphoreType.DMA((2, comps)),
+            pltpu.SemaphoreType.DMA((2,)),
             pltpu.SemaphoreType.DMA((2,)),
             pltpu.SemaphoreType.REGULAR((max(n_lat, n_rad).bit_length(),)),
         ],

time: 28.3 us -> 26.9 us (0.951)
  Pallas kernels: 27.5 us -> 26.1 us
    pallas_call x1, Pallas kernels: 26.6 us -> 25.2 us  [on_device(): pl.pallas_call(functools.partial(kernel, n_lat, n_rad, n_steps, n_prev, c...]
where the time goes in v4:
time: 26.9 us; the launch traced here: 26.7 us
  Pallas kernels  26.1 us (97%)
  between operations  0.64 us (2%)
    pallas_call x1, Pallas kernels, on_device(): pl.pallas_call(functools.partial(kernel, n_lat, n_rad, n_steps, n_prev, c...  25.2 us
    pallas_call x1, Pallas kernels, on_device(): pl.pallas_call(store, out_shape=(jax.ShapeDtypeStruct(out.shape, F32), ja...  0.9 us

profile of v4, /device:TPU:0, one launch (start us, length us, event | category | flops | bytes accessed | tf_op | source)
XLA Modules:
  0.0 26.7 jit_solution(8895062069259875691)
XLA Ops:
  0.6 25.2 %shard_map.68 = (f32[4,192,256]{2,1,0:T(8,128)S(1)}, f32[9,9]{1,0:T(8,128)S(1)}) custom-call(f32[192,256]{1,0:T(8,128)} %bitcast.4, f32[4,192,256]{2,1,0:T(8,128)} %bitcast.3, s32[4,4,128]{2,1,0:T(4,128)} %ids_hbm.1, f32[8]{0:T(128)} %visc_hbm.1, f32[4]{0:T(128)} %shift_hbm.1), custom_call_target="tpu_custom_call" | custom-call | tf_op jit(solution)/shard_map/pallas_call | solution.py:824
  25.8 0.9 %shard_map.69 = (f32[4,192,256]{2,1,0:T(8,128)}, f32[9,9]{1,0:T(8,128)}) custom-call(f32[4,192,256]{2,1,0:T(8,128)S(1)} %get-tuple-element.6.vec_ref, f32[9,9]{1,0:T(8,128)S(1)} %get-tuple-element.7.gram_ref), custom_call_target="tpu_custom_call" | custom-call | tf_op jit(solution)/shard_map/pallas_call | solution.py:877

commit v5 on v4

--- a/solution.py
+++ b/solution.py
@@ -22,8 +22,8 @@
 ROWS_X, ROWS_G, ROWS_A, ROWS_C = 0, 8, 12, 16
 RIM = (
     ((1, 0), (0, 8), (4, 4), ROWS_X, 0),
+    ((0, 1), (8, 8), (4, 4), ROWS_X, 4),
     ((1, 0), (16, 4), (7, 1), ROWS_G, 3),
-    ((0, 1), (8, 8), (4, 4), ROWS_X, 4),
     ((0, 1), (20, 4), (7, 1), ROWS_G, 7),
     ((1, 1), (24, 4), (7, 1), ROWS_C, 0),
     ((1, 1), (28, 4), (7, 1), ROWS_C, 4),
@@ -326,8 +326,17 @@
                 device_id_type=MESH,
             ).start()
 
+    def start_layers(c):
+        for d, (first, count), (row, high), to, to_row in RIM[:2]:
+            remote(
+                rim_send.at[c, pl.ds(first, count), pl.ds(row, high)],
+                rim_recv.at[c, pl.ds(to, count), pl.ds(to_row, high)],
+                rim_sems.at[0],
+                d,
+            )
+
     def start_rim():
-        for d, (first, count), (row, high), to, to_row in RIM:
+        for d, (first, count), (row, high), to, to_row in RIM[2:]:
             remote(
                 rim_send.at[:, pl.ds(first, count), pl.ds(row, high)],
                 rim_recv.at[:, pl.ds(to, count), pl.ds(to_row, high)],
@@ -714,19 +723,21 @@
         split_columns(i)
 
     total = jnp.zeros((1, half_y), F32)
-    for k in range(n_steps):
+    for k in range(n_steps - 1):
         for c in range(comps):
             finish_round(k, c)
             absorb(k, c)
             apply(k, c)
-            if k + 1 < n_steps:
-                start_round(k + 1, c)
+            start_round(k + 1, c)
+            if k == n_steps - 2:
+                if c:
+                    start_layers(c - 1)
+                pack_rim(c)
+        if k == n_steps - 2:
+            start_layers(comps - 1)
+            start_rim()
         if k == 0:
             start_eta()
-        if k == n_steps - 2:
-            for c in range(comps):
-                pack_rim(c)
-            start_rim()
         if k >= 2:
             take_token(k - 2)
         if k >= 1:
@@ -746,14 +757,18 @@
                 rim_scaled[0, i] = eta_recv[0] * weight(*key)
                 rim_scaled[1, i] = tip_eta * weight(*key)
     assert n_steps >= 2
-    for j in range(n_steps - 2, len(reaches)):
-        take_token(j)
-        send_token(j + 1)
-    for c in range(comps):
-        own_planes(c)
-        to_native(n_steps, c)
+    k = n_steps - 1
+    per = rows // 8 // comps
+    whole = gram_zero(n_vec - 2)
     acc = gram_zero(n_vec - 1)
     for c in range(comps):
+        finish_round(k, c)
+        absorb(k, c)
+        apply(k, c)
+        own_planes(c)
+        to_native(k, c)
+        to_native(n_steps, c)
+        whole = gram_part(n_vec - 2, whole, c * per, per)
         acc = lax.fori_loop(
             8 * c + 1,
             8 * c + 8,
@@ -763,6 +778,10 @@
             acc,
             unroll=7,
         )
+    total = total + gram_close(n_vec - 2, whole)
+    for j in range(max(k - 2, 0), len(reaches)):
+        take_token(j)
+        send_token(j + 1)
     settle(rim_sems.at[0], opposite(rim_sizes))
     add_rim()
     for c in range(comps):
@@ -784,6 +803,7 @@
         ).start()
 
     each_other(scatter)
+    write_out(n_steps - 1)
     write_out(n_steps)
     sent = [size for step in range(n_steps) for size in round_sizes(step)] * comps
     settle(send_sem.at[0], sent + rim_sizes + eta_sizes)
@@ -796,10 +816,9 @@
 
 
 def store(vec_ref, gram_ref, vec_out, gram_out, sems):
-    copies = [
-        pltpu.make_async_copy(vec_ref, vec_out, sems.at[0]),
-        pltpu.make_async_copy(gram_ref, gram_out, sems.at[1]),
-    ]
+    copies = [pltpu.make_async_copy(gram_ref, gram_out, sems.at[0])]
+    for i in range(vec_ref.shape[0]):
+        copies.append(pltpu.make_async_copy(vec_ref.at[i], vec_out.at[i], sems.at[1 + i]))
     for copy in copies:
         copy.start()
     for copy in copies:
@@ -882,7 +901,7 @@
         ),
         in_specs=[vmem_spec] * 2,
         out_specs=(hbm_spec, hbm_spec),
-        scratch_shapes=[pltpu.SemaphoreType.DMA((2,))],
+        scratch_shapes=[pltpu.SemaphoreType.DMA((1 + n_steps,))],
     )(*(pltpu.with_memory_space_constraint(a, pltpu.VMEM) for a in (out, gram)))
     return out.reshape((n_steps,) + residual.shape), gram
 

time: 26.9 us -> 26.9 us (level)
  no operation moved by 1% of the time
where the time goes in v5:
time: 26.9 us; the launch traced here: 26.7 us
  Pallas kernels  26.1 us (97%)
  between operations  0.64 us (2%)
    pallas_call x1, Pallas kernels, on_device(): pl.pallas_call(functools.partial(kernel, n_lat, n_rad, n_steps, n_prev, c...  25.2 us
    pallas_call x1, Pallas kernels, on_device(): pl.pallas_call(store, out_shape=(jax.ShapeDtypeStruct(out.shape, F32), ja...  0.92 us

profile of v5, /device:TPU:0, one launch (start us, length us, event | category | flops | bytes accessed | tf_op | source)
XLA Modules:
  0.0 26.7 jit_solution(8587490361287164100)
XLA Ops:
  0.6 25.2 %shard_map.68 = (f32[4,192,256]{2,1,0:T(8,128)S(1)}, f32[9,9]{1,0:T(8,128)S(1)}) custom-call(f32[192,256]{1,0:T(8,128)} %bitcast.4, f32[4,192,256]{2,1,0:T(8,128)} %bitcast.3, s32[4,4,128]{2,1,0:T(4,128)} %ids_hbm.1, f32[8]{0:T(128)} %visc_hbm.1, f32[4]{0:T(128)} %shift_hbm.1), custom_call_target="tpu_custom_call" | custom-call | tf_op jit(solution)/shard_map/pallas_call | solution.py:843
  25.8 0.9 %shard_map.69 = (f32[4,192,256]{2,1,0:T(8,128)}, f32[9,9]{1,0:T(8,128)}) custom-call(f32[4,192,256]{2,1,0:T(8,128)S(1)} %get-tuple-element.6.vec_ref, f32[9,9]{1,0:T(8,128)S(1)} %get-tuple-element.7.gram_ref), custom_call_target="tpu_custom_call" | custom-call | tf_op jit(solution)/shard_map/pallas_call | solution.py:896

commit v6 on v5

--- a/solution.py
+++ b/solution.py
@@ -29,6 +29,26 @@
     ((1, 1), (28, 4), (7, 1), ROWS_C, 4),
     ((1, -1), (32, 4), (4, 1), ROWS_A, 3),
     ((-1, 1), (36, 4), (3, 1), ROWS_A, 7),
+)
+EDGE_T, EDGE_U, EDGE_H, EDGE_G = 0, 4, 8, 20
+EDGES = (
+    ((-1, -1), (8, 6), EDGE_H, 0),
+    ((-1, -1), (14, 6), EDGE_H, 4),
+    ((-1, 0), (8, 6), EDGE_H + 6, 0),
+    ((0, -1), (14, 6), EDGE_H + 6, 4),
+    ((1, 0), (0, 4), EDGE_T, 0),
+    ((0, 1), (4, 4), EDGE_U, 0),
+    ((1, -1), (0, 4), EDGE_G, 0),
+    ((-1, 1), (4, 4), EDGE_G, 4),
+)
+ETAS = (
+    ((-1, 0), 2, 0, 3, 2, 0),
+    ((0, -1), 2, 4, 3, 2, 4),
+    ((1, 0), 0, 4, 4, 0, 0),
+    ((0, 1), 1, 4, 4, 0, 4),
+    ((1, 1), 0, 7, 1, 1, 0),
+    ((-1, 1), 2, 0, 3, 3, 0),
+    ((1, -1), 2, 4, 3, 3, 4),
 )
 
 
@@ -86,6 +106,8 @@
     rim_recv,
     block_send,
     block_recv,
+    edge_send,
+    edge_recv,
     eta_send,
     eta_recv,
     rim_scaled,
@@ -149,6 +171,8 @@
                     device_id_type=MESH,
                 )
 
+    for ref in (edge_recv, eta_recv):
+        ref[...] = jnp.zeros_like(ref)
     signal_around(barrier, 1, LAST)
 
     for d in DIRS:
@@ -163,8 +187,11 @@
         def _(ref=ref, slot=slot):
             ref[:, :, slot] = jnp.zeros(ref.shape[:2] + ref.shape[3:], F32)
 
-    for ref in (rim_recv, block_recv, eta_recv):
+    for ref in (rim_recv, block_recv):
         ref[...] = jnp.zeros_like(ref)
+
+    for ref in (ghost_r, ghost_x, ghost_c):
+        ref[0] = jnp.zeros(ref.shape[1:], F32)
 
     reaches = []
     while (2 << len(reaches)) < max(n_lat, n_rad) - 1:
@@ -258,7 +285,7 @@
             src_ref=a,
             dst_ref=b,
             send_sem=send_sem.at[0],
-            recv_sem=recv_sem.at[step % 2, c],
+            recv_sem=recv_sem.at[step % 3, c],
             device_id={"lat": lat + d[1], "rad": rad + d[0]},
             device_id_type=MESH,
         )
@@ -269,8 +296,10 @@
         wanted = FIRST if step == 0 else DIRS
         return [d for d in order if d in wanted]
 
-    def start_round(step, c):
+    def start_round(step, c, among=DIRS):
         for d in dirs_of(step):
+            if d not in among:
+                continue
 
             @pl.when(within(*d))
             def _(d=d):
@@ -309,10 +338,11 @@
 
     rim_sizes = [(d, comps * count * high) for d, (_, count), (_, high), _, _ in RIM]
     rim_sizes.append(((1, 1), comps * 8))
-    eta_sizes = [((1, 0), 4), ((0, 1), 4), ((1, 1), 1)]
+    edge_sizes = [(d, comps * count) for d, (_, count), _, _ in EDGES]
+    edge_sizes += [(d, high) for d, _, _, high, _, _ in ETAS]
 
     def finish_round(step, c):
-        settle(recv_sem.at[step % 2, c], opposite(round_sizes(step)))
+        settle(recv_sem.at[step % 3, c], opposite(round_sizes(step)))
 
     def remote(a, b, recv, d):
         @pl.when(within(*d))
@@ -347,18 +377,25 @@
             block_send.at[:, pl.ds(0, comps)], block_recv.at[:, pl.ds(0, comps)], rim_sems.at[0], (1, 1)
         )
 
-    def start_eta():
-        for d, slot, row, high, to, to_row in (
-            ((1, 0), 0, 4, 4, 0, 0),
-            ((0, 1), 1, 4, 4, 0, 4),
-            ((1, 1), 0, 7, 1, 1, 0),
-        ):
-            remote(
-                eta_send.at[slot, pl.ds(row, high)],
-                eta_recv.at[to, pl.ds(to_row, high)],
-                rim_sems.at[1],
-                d,
-            )
+    def start_edges(among):
+        for d, (first, count), to, to_row in EDGES:
+            if d in among:
+                remote(
+                    edge_send.at[pl.ds(first, count), pl.ds(0, comps)],
+                    edge_recv.at[pl.ds(to, count), pl.ds(to_row, comps)],
+                    rim_sems.at[1],
+                    d,
+                )
+
+    def start_etas(among):
+        for d, slot, row, high, to, to_row in ETAS:
+            if d in among:
+                remote(
+                    eta_send.at[slot, pl.ds(row, high)],
+                    eta_recv.at[to, pl.ds(to_row, high)],
+                    rim_sems.at[1],
+                    d,
+                )
 
     def pack_x(vals, at):
         out = None
@@ -385,7 +422,7 @@
         moved = jnp.where(sub == 6, roll_s(low, -1), high)
         return jnp.where(sub == 4, roll_s(low, 1), jnp.where(sub == 5, roll_s(high, 2), moved))
 
-    def apply(k, c):
+    def apply(k, c, send=True, hold=True):
         s = shift_ref[k]
         cur = k % 2
         new = 1 - cur
@@ -434,12 +471,13 @@
                 res[0, p, q] = res[0, p, q] + keep(upper, roll_s(res[4, p, q], 4))
             px[0, q] = px[0, q] + keep(upper, roll_s(px[4, q], 4))
         step = k + 1
-        last = step == n_steps
+        send = send and step < n_steps
+        ghosts = hold and step < n_steps
         for q in range(2):
             face = slice(8 * q, 8 * q + 8)
             edge = slice(16 + q, 17 + q)
             row = slice(q, q + 1)
-            if not last:
+            if send:
                 send_r[step, c, 1, face] = jnp.where(upper, res[4, 1, q], roll_s(res[4, 0, q], 4))
                 send_r[step, c, 1, edge] = px[4, q][7:8]
                 send_x[step, c, 1, face] = pack_x([px[ro, q] for ro in range(4)], 3)
@@ -452,12 +490,12 @@
                 send_c[step, c, 0, row] = res[0, 0, q][0:1]
                 send_c[step, c, 1, row] = px[0, q][3:4]
                 send_c[step, c, 2, row] = res[4, 0, q][4:5]
-            for ro in range(4):
+            for ro in range(4 if hold else 0):
                 for p in range(2):
                     vec[new, c, ro, p, q] = res[ro, p, q] - s * u[ro, p, q]
-                if not last:
+                if ghosts:
                     ghost_x[new, c, ro, q] = px[ro, q] - s * gx[ro, q]
-            if not last:
+            if ghosts:
                 for p in range(2):
                     ghost_r[new, c, p, q] = res[4, p, q] - s * u[4, p, q]
                 ghost_c[new, c, q] = px[4, q] - s * gx[4, q]
@@ -485,8 +523,7 @@
     group_last = lax.rem(sub, 4) == 3
     group_first = lax.rem(sub, 4) == 0
 
-    def own_planes(c):
-        cur = (n_steps - 1) % 2
+    def own_planes(c, cur):
         for q in range(2):
             side = jnp.where(corner3, ghost_x[cur, c, 0, q], roll_s(ghost_r[cur, c, 0, q], 3))
             for p in range(2):
@@ -498,23 +535,94 @@
                 if p == 0:
                     rim_own[c, 4 + q] = jnp.where(group_last, side, roll_s(plane, -1))
 
-    def rim_elements(u, scale):
+    def across(u):
         t = {}
         for p in range(3):
             for q in range(2):
                 t[0, p, q], t[1, p, q], t[2, p, q] = forward(u[0, p, q], u[1, p, q], u[2, p, q])
+        return t
+
+    def rim_elements(t, scale, upper_plane=True, only_end=False):
         w = {}
         for a in range(3):
             x = {}
             for q in range(2):
-                x[0, q], x[1, q], x[2, q] = forward(t[a, 0, q], t[a, 1, q], t[a, 2, q])
+                if only_end:
+                    end = t[a, 2, q]
+                    x[0, q], x[1, q], x[2, q] = end, -end, end
+                else:
+                    x[0, q], x[1, q], x[2, q] = forward(t[a, 0, q], t[a, 1, q], t[a, 2, q])
             for b in range(3):
                 x[b, 0], x[b, 1] = y_pass(x[b, 0], x[b, 1], a, b, scale)
             for q in range(2):
                 w[a, 0, q], w[a, 1, q], w[a, 2, q] = backward(x[0, q], x[1, q], x[2, q])
+        sign = -1.0 if upper_plane else 1.0
         return {
-            (p, q): w[0, p, q] + w[2, p, q] - w[1, p, q] for p in range(3) for q in range(2)
+            (p, q): w[0, p, q] + w[2, p, q] + (w[1, p, q] if sign > 0 else -w[1, p, q])
+            for p in range(3)
+            for q in range(2)
         }
+
+    def add_planes(new, c, side, tip):
+        for q in range(2):
+            out = [side[0, q] + keep(~group_first, roll_s(side[2, q], 1)), side[1, q]]
+            for p in range(2):
+                for e in range(2):
+                    ro = 2 * e + p
+                    add = keep(corner4, roll_s(out[p], -(2 + e)))
+                    add = jnp.where(corner0, roll_s(out[p], -(4 + e)), add)
+                    if ro == 0:
+                        add = add + keep(~upper, out[0]) + keep(corner0, roll_s(tip[2, q], -c))
+                    vec[new, c, ro, 0, q] += add
+            vec[new, c, 0, 1, q] += keep(~upper, out[1])
+
+    def add_first():
+        sides = {}
+        corner = {}
+        zero = jnp.zeros((8, half_y), F32)
+        for c in range(comps):
+            own_planes(c, 0)
+            t = {}
+            for q in range(2):
+                u = [keep(group_last, roll_s(edge_recv[EDGE_G + 2 * n + q], 3 - c)) for n in range(2)]
+                for p in range(2):
+                    plane = rim_own[c, 2 * p + q]
+                    t[0, p, q], t[1, p, q], t[2, p, q] = plane, -plane, plane
+                    if p == 0:
+                        part = keep(sub == c, roll_s(plane, c))
+                        corner[2, 2, q] = corner[2, 2, q] + part if c else part
+                t[0, 2, q], t[1, 2, q], t[2, 2, q] = forward(u[0], u[1], rim_own[c, 4 + q])
+            sides[c] = rim_elements(t, lambda i: rim_scaled[0, i])
+        for q in range(2):
+            for n in range(2):
+                corner[n, 2, q] = edge_recv[EDGE_T + 2 * n + q]
+                corner[2, n, q] = edge_recv[EDGE_U + 2 * n + q]
+                for p in range(2):
+                    corner[n, p, q] = zero
+        tip = rim_elements(across(corner), lambda i: rim_scaled[1, i])
+        high = []
+        for g in range(2):
+            t = {}
+            for q in range(2):
+                t[0, 2, q], t[1, 2, q], t[2, 2, q] = forward(
+                    *(edge_recv[EDGE_H + 6 * g + 2 * n + q] for n in range(3))
+                )
+            high.append(rim_elements(t, lambda i, g=g: rim_scaled[2 + g, i], False, True))
+        for c in range(comps):
+            add_planes(1, c, sides[c], tip)
+            for q in range(2):
+                far = sides[c][2, q]
+                ghost_x[1, c, 0, q] += keep(corner3, far + roll_s(high[1][2, q], -1 - c))
+                ghost_r[1, c, 0, q] += (
+                    keep(corner4, roll_s(far, -3) + roll_s(high[1][2, q], 4 - c))
+                    + keep(corner7, roll_s(high[0][0, q], 7 - c))
+                )
+                ghost_r[1, c, 1, q] += keep(corner7, roll_s(high[0][1, q], 7 - c))
+                for t in range(2):
+                    ghost_x[1, c, 2 + t, q] += keep(corner7, roll_s(high[0][t, q], 3 - c))
+                ghost_c[1, c, q] += keep(
+                    corner7, roll_s(high[0][2, q], 7 - c) + roll_s(high[0][2, q], 3 - c)
+                )
 
     def add_rim():
         cur = (n_steps - 1) % 2
@@ -542,27 +650,14 @@
                     part = keep(sub == c, part)
                     key = key + (q,)
                     corner[key] = corner[key] + part if c else part
-            sides[c] = rim_elements(u, lambda i: rim_scaled[0, i])
+            sides[c] = rim_elements(across(u), lambda i: rim_scaled[0, i])
         for q in range(2):
             for n in range(2):
                 for p in range(2):
                     corner[n, p, q] = block_recv[4 * n + 2 * p + q]
-        tip = rim_elements(corner, lambda i: rim_scaled[1, i])
+        tip = rim_elements(across(corner), lambda i: rim_scaled[1, i])
         for c in range(comps):
-            for q in range(2):
-                out = [
-                    sides[c][0, q] + keep(~group_first, roll_s(sides[c][2, q], 1)),
-                    sides[c][1, q],
-                ]
-                for p in range(2):
-                    for e in range(2):
-                        ro = 2 * e + p
-                        add = keep(corner4, roll_s(out[p], -(2 + e)))
-                        add = jnp.where(corner0, roll_s(out[p], -(4 + e)), add)
-                        if ro == 0:
-                            add = add + keep(~upper, out[0]) + keep(corner0, roll_s(tip[2, q], -c))
-                        vec[new, c, ro, 0, q] += add
-                vec[new, c, 0, 1, q] += keep(~upper, out[1])
+            add_planes(new, c, sides[c], tip)
 
     def absorb(step, c):
         new = step % 2
@@ -690,13 +785,22 @@
             send_r[0, c, 0, face] = edge[16 * c : 16 * c + 8, lanes]
             send_x[0, c, 0, face] = edge[16 * c + 8 : 16 * c + 16, lanes]
             send_c[0, c, 0, q : q + 1] = edge[16 * c : 16 * c + 1, lanes]
+            along = [8 + 6, 8 + 7, 3, 7, 8, 9, 10, 0, 4, 1]
+            for slot, row in enumerate(along):
+                at = 16 * c + row
+                edge_send[2 * slot + q, c : c + 1] = edge[at : at + 1, lanes]
+
+    hello = token_sem.at[token_sem.shape[0] - 1]
+    others = tuple(d for d in DIRS if d not in FIRST)
 
     @pl.when(jnp.logical_or(rad > 0, lat > 0))
     def _():
         pl.semaphore_wait(barrier, around(1, FIRST))
 
+    signal_around(hello, 1, FIRST)
     for c in range(comps):
         start_round(0, c)
+    start_edges(FIRST)
     split_columns(n_prev)
     for c in range(comps):
         for ro in range(4):
@@ -718,12 +822,44 @@
             scaled[e, i] = eta * weight(*key)
     eta_send[0] = etas[1]
     eta_send[1] = to_column(*etas)
+    eta_send[2] = jnp.where(
+        upper,
+        jnp.broadcast_to(etas[1][4:5], (8, half_y)),
+        jnp.broadcast_to(etas[0][3:4], (8, half_y)),
+    )
+    start_etas(FIRST)
+    for c in range(comps):
+        apply(0, c, hold=False)
+        if c < comps - 1:
+            start_round(1, c, FIRST)
+
+    @pl.when(jnp.logical_or(rad < n_rad - 1, lat < n_lat - 1))
+    def _():
+        pl.semaphore_wait(hello, around(1, LAST))
+
+    for c in range(comps):
+        start_round(1, c, others if c < comps - 1 else DIRS)
+    start_edges(others)
+    start_etas(others)
+
+    total = jnp.zeros((1, half_y), F32)
     prev_copy.wait()
     for i in range(n_prev):
         split_columns(i)
-
-    total = jnp.zeros((1, half_y), F32)
-    for k in range(n_steps - 1):
+    for i in range(n_prev + 1):
+        total = total + gram_row(i)
+
+    for c in range(comps):
+        finish_round(0, c)
+        absorb(0, c)
+        apply(0, c, send=False)
+    settle(rim_sems.at[1], opposite(edge_sizes))
+    tip_eta = jnp.broadcast_to(eta_recv[1, 0:1], (8, half_y))
+    for key, i in kinds.items():
+        for slot in range(4):
+            rim_scaled[slot, i] = (tip_eta if slot == 1 else eta_recv[slot]) * weight(*key)
+    add_first()
+    for k in range(1, n_steps - 1):
         for c in range(comps):
             finish_round(k, c)
             absorb(k, c)
@@ -736,27 +872,14 @@
         if k == n_steps - 2:
             start_layers(comps - 1)
             start_rim()
-        if k == 0:
-            start_eta()
         if k >= 2:
             take_token(k - 2)
-        if k >= 1:
-            send_token(k - 1)
-        if k == 0:
-            for i in range(n_prev + 1):
-                total = total + gram_row(i)
-        else:
-            for c in range(comps):
-                to_native(k, c)
-            write_out(k)
-            total = total + gram_row(n_prev + k)
-        if k == n_steps - 2:
-            settle(rim_sems.at[1], opposite(eta_sizes))
-            tip_eta = jnp.broadcast_to(eta_recv[1, 0:1], (8, half_y))
-            for key, i in kinds.items():
-                rim_scaled[0, i] = eta_recv[0] * weight(*key)
-                rim_scaled[1, i] = tip_eta * weight(*key)
-    assert n_steps >= 2
+        send_token(k - 1)
+        for c in range(comps):
+            to_native(k, c)
+        write_out(k)
+        total = total + gram_row(n_prev + k)
+    assert n_steps >= 3
     k = n_steps - 1
     per = rows // 8 // comps
     whole = gram_zero(n_vec - 2)
@@ -765,7 +888,7 @@
         finish_round(k, c)
         absorb(k, c)
         apply(k, c)
-        own_planes(c)
+        own_planes(c, k % 2)
         to_native(k, c)
         to_native(n_steps, c)
         whole = gram_part(n_vec - 2, whole, c * per, per)
@@ -806,7 +929,7 @@
     write_out(n_steps - 1)
     write_out(n_steps)
     sent = [size for step in range(n_steps) for size in round_sizes(step)] * comps
-    settle(send_sem.at[0], sent + rim_sizes + eta_sizes)
+    settle(send_sem.at[0], sent + rim_sizes + edge_sizes)
     for i in range(2):
         pltpu.make_async_copy(gram_recv, gram_recv, gram_sems.at[i]).wait()
     full = (total + jnp.sum(gram_recv[...], axis=0)) * (1.0 / (rows * 2 * half_y * n_dev))
@@ -872,13 +995,15 @@
             vmem((comps, 20) + tile, F32),
             vmem((8,) + tile, F32),
             vmem((8,) + tile, F32),
-            vmem((2,) + tile, F32),
-            vmem((2,) + tile, F32),
-            vmem((2, 9) + tile, F32),
+            vmem((20,) + tile, F32),
+            vmem((24,) + tile, F32),
+            vmem((3,) + tile, F32),
+            vmem((4,) + tile, F32),
+            vmem((4, 9) + tile, F32),
             vmem((comps, 6) + tile, F32),
             pltpu.SemaphoreType.DMA((5,)),
             pltpu.SemaphoreType.DMA((1,)),
-            pltpu.SemaphoreType.DMA((2, comps)),
+            pltpu.SemaphoreType.DMA((3, comps)),
             pltpu.SemaphoreType.DMA((2,)),
             pltpu.SemaphoreType.DMA((2,)),
             pltpu.SemaphoreType.REGULAR((max(n_lat, n_rad).bit_length(),)),

time: 26.9 us -> 26 us (0.967)
  Pallas kernels: 26.1 us -> 25.2 us
    pallas_call x1, Pallas kernels: 25.2 us -> 24.3 us  [on_device(): pl.pallas_call(functools.partial(kernel, n_lat, n_rad, n_steps, n_prev, c...]
where the time goes in v6:
time: 26 us; the launch traced here: 25.9 us
  Pallas kernels  25.2 us (97%)
  between operations  0.64 us (2%)
    pallas_call x1, Pallas kernels, on_device(): pl.pallas_call(functools.partial(kernel, n_lat, n_rad, n_steps, n_prev, c...  24.3 us
    pallas_call x1, Pallas kernels, on_device(): pl.pallas_call(store, out_shape=(jax.ShapeDtypeStruct(out.shape, F32), ja...  0.92 us

profile of v6, /device:TPU:0, one launch (start us, length us, event | category | flops | bytes accessed | tf_op | source)
XLA Modules:
  0.0 25.9 jit_solution(11941377766375966051)
XLA Ops:
  0.6 24.3 %shard_map.68 = (f32[4,192,256]{2,1,0:T(8,128)S(1)}, f32[9,9]{1,0:T(8,128)S(1)}) custom-call(f32[192,256]{1,0:T(8,128)} %bitcast.4, f32[4,192,256]{2,1,0:T(8,128)} %bitcast.3, s32[4,4,128]{2,1,0:T(4,128)} %ids_hbm.1, f32[8]{0:T(128)} %visc_hbm.1, f32[4]{0:T(128)} %shift_hbm.1), custom_call_target="tpu_custom_call" | custom-call | tf_op jit(solution)/shard_map/pallas_call | solution.py:966
  25.0 0.9 %shard_map.69 = (f32[4,192,256]{2,1,0:T(8,128)}, f32[9,9]{1,0:T(8,128)}) custom-call(f32[4,192,256]{2,1,0:T(8,128)S(1)} %get-tuple-element.6.vec_ref, f32[9,9]{1,0:T(8,128)S(1)} %get-tuple-element.7.gram_ref), custom_call_target="tpu_custom_call" | custom-call | tf_op jit(solution)/shard_map/pallas_call | solution.py:1021

commit v7 on v6

--- a/solution.py
+++ b/solution.py
@@ -192,6 +192,20 @@
 
     for ref in (ghost_r, ghost_x, ghost_c):
         ref[0] = jnp.zeros(ref.shape[1:], F32)
+
+    hello = token_sem.at[token_sem.shape[0] - 1]
+    hello_far = token_sem.at[token_sem.shape[0] - 2]
+
+    def answer():
+        @pl.when(jnp.logical_or(rad > 0, lat > 0))
+        def _():
+            pl.semaphore_wait(barrier, around(1, FIRST))
+
+        signal_around(hello, 1, FIRST[:2])
+        signal_around(hello_far, 1, FIRST[2:])
+
+    soon = jnp.logical_or(rad == 0, lax.rem(rad, 2) == 1)
+    pl.when(soon)(answer)
 
     reaches = []
     while (2 << len(reaches)) < max(n_lat, n_rad) - 1:
@@ -790,14 +804,7 @@
                 at = 16 * c + row
                 edge_send[2 * slot + q, c : c + 1] = edge[at : at + 1, lanes]
 
-    hello = token_sem.at[token_sem.shape[0] - 1]
-    others = tuple(d for d in DIRS if d not in FIRST)
-
-    @pl.when(jnp.logical_or(rad > 0, lat > 0))
-    def _():
-        pl.semaphore_wait(barrier, around(1, FIRST))
-
-    signal_around(hello, 1, FIRST)
+    pl.when(jnp.logical_not(soon))(answer)
     for c in range(comps):
         start_round(0, c)
     start_edges(FIRST)
@@ -830,22 +837,30 @@
     start_etas(FIRST)
     for c in range(comps):
         apply(0, c, hold=False)
-        if c < comps - 1:
-            start_round(1, c, FIRST)
+        start_round(1, c, FIRST)
 
     @pl.when(jnp.logical_or(rad < n_rad - 1, lat < n_lat - 1))
     def _():
-        pl.semaphore_wait(hello, around(1, LAST))
-
-    for c in range(comps):
-        start_round(1, c, others if c < comps - 1 else DIRS)
+        pl.semaphore_wait(hello, around(1, LAST[:2]))
+
+    others = tuple(d for d in DIRS if d not in FIRST and d not in LAST[2:])
     start_edges(others)
     start_etas(others)
+    for c in range(comps):
+        start_round(1, c, others)
 
     total = jnp.zeros((1, half_y), F32)
     prev_copy.wait()
     for i in range(n_prev):
         split_columns(i)
+
+    @pl.when(jnp.logical_and(rad < n_rad - 1, lat < n_lat - 1))
+    def _():
+        pl.semaphore_wait(hello_far, 1)
+
+    start_etas(LAST[2:])
+    for c in range(comps):
+        start_round(1, c, LAST[2:])
     for i in range(n_prev + 1):
         total = total + gram_row(i)
 
@@ -872,9 +887,8 @@
         if k == n_steps - 2:
             start_layers(comps - 1)
             start_rim()
-        if k >= 2:
-            take_token(k - 2)
-        send_token(k - 1)
+        if k == n_steps - 2:
+            send_token(0)
         for c in range(comps):
             to_native(k, c)
         write_out(k)
@@ -888,6 +902,9 @@
         finish_round(k, c)
         absorb(k, c)
         apply(k, c)
+        if c == 0:
+            take_token(0)
+            send_token(1)
         own_planes(c, k % 2)
         to_native(k, c)
         to_native(n_steps, c)
@@ -902,9 +919,6 @@
             unroll=7,
         )
     total = total + gram_close(n_vec - 2, whole)
-    for j in range(max(k - 2, 0), len(reaches)):
-        take_token(j)
-        send_token(j + 1)
     settle(rim_sems.at[0], opposite(rim_sizes))
     add_rim()
     for c in range(comps):
@@ -925,6 +939,9 @@
             device_id_type=MESH,
         ).start()
 
+    for j in range(1, len(reaches)):
+        take_token(j)
+        send_token(j + 1)
     each_other(scatter)
     write_out(n_steps - 1)
     write_out(n_steps)

time: 26 us -> 25.8 us (level)
    pallas_call x1, Pallas kernels: 24.3 us -> 24 us  [on_device(): pl.pallas_call(functools.partial(kernel, n_lat, n_rad, n_steps, n_prev, c...]
where the time goes in v7:
time: 25.8 us; the launch traced here: 25.6 us
  Pallas kernels  25 us (97%)
  between operations  0.64 us (2%)
    pallas_call x1, Pallas kernels, on_device(): pl.pallas_call(functools.partial(kernel, n_lat, n_rad, n_steps, n_prev, c...  24 us
    pallas_call x1, Pallas kernels, on_device(): pl.pallas_call(store, out_shape=(jax.ShapeDtypeStruct(out.shape, F32), ja...  0.92 us

profile of v7, /device:TPU:0, one launch (start us, length us, event | category | flops | bytes accessed | tf_op | source)
XLA Modules:
  0.0 25.6 jit_solution(3480043712777174351)
XLA Ops:
  0.6 24.0 %shard_map.68 = (f32[4,192,256]{2,1,0:T(8,128)S(1)}, f32[9,9]{1,0:T(8,128)S(1)}) custom-call(f32[192,256]{1,0:T(8,128)} %bitcast.4, f32[4,192,256]{2,1,0:T(8,128)} %bitcast.3, s32[4,4,128]{2,1,0:T(4,128)} %ids_hbm.1, f32[8]{0:T(128)} %visc_hbm.1, f32[4]{0:T(128)} %shift_hbm.1), custom_call_target="tpu_custom_call" | custom-call | tf_op jit(solution)/shard_map/pallas_call | solution.py:983
  24.7 0.9 %shard_map.69 = (f32[4,192,256]{2,1,0:T(8,128)}, f32[9,9]{1,0:T(8,128)}) custom-call(f32[4,192,256]{2,1,0:T(8,128)S(1)} %get-tuple-element.6.vec_ref, f32[9,9]{1,0:T(8,128)S(1)} %get-tuple-element.7.gram_ref), custom_call_target="tpu_custom_call" | custom-call | tf_op jit(solution)/shard_map/pallas_call | solution.py:1038

commit v8 on v7

--- a/solution.py
+++ b/solution.py
@@ -157,12 +157,19 @@
                 ok = one if ok is None else jnp.logical_and(ok, one)
         return ok
 
-    def signal_around(sem, far, dirs):
+    even = lax.rem(lat, 2) == 0
+    odd = jnp.logical_not(even)
+
+    def allowed(d, when):
+        ok = within(*d)
+        return ok if when is None else jnp.logical_and(ok, when)
+
+    def signal_around(sem, far, dirs, when=None):
         for dr, dx in dirs:
             if (dr and n_rad <= far) or (dx and n_lat <= far):
                 continue
 
-            @pl.when(within(dr * far, dx * far))
+            @pl.when(allowed((dr * far, dx * far), when))
             def _(dr=dr, dx=dx):
                 pl.semaphore_signal(
                     sem,
@@ -174,6 +181,8 @@
     for ref in (edge_recv, eta_recv):
         ref[...] = jnp.zeros_like(ref)
     signal_around(barrier, 1, LAST)
+    signal_around(barrier, 1, ((-1, 0),), even)
+    signal_around(barrier, 1, ((0, -1), (-1, -1), (-1, 1), (1, -1)), odd)
 
     for d in DIRS:
         if d in R_DIRS:
@@ -197,14 +206,19 @@
     hello_far = token_sem.at[token_sem.shape[0] - 2]
 
     def answer():
-        @pl.when(jnp.logical_or(rad > 0, lat > 0))
+        @pl.when(even)
+        def _():
+            pl.semaphore_wait(barrier, around(1, DIRS))
+
+        @pl.when(odd)
         def _():
             pl.semaphore_wait(barrier, around(1, FIRST))
 
-        signal_around(hello, 1, FIRST[:2])
-        signal_around(hello_far, 1, FIRST[2:])
-
-    soon = jnp.logical_or(rad == 0, lax.rem(rad, 2) == 1)
+        signal_around(hello, 1, ((-1, 0),), odd)
+        signal_around(hello, 1, ((0, -1),), even)
+        signal_around(hello_far, 1, ((-1, -1),), even)
+
+    soon = jnp.logical_and(odd, jnp.logical_or(rad == 0, lax.rem(rad, 2) == 1))
     pl.when(soon)(answer)
 
     reaches = []
@@ -310,12 +324,12 @@
         wanted = FIRST if step == 0 else DIRS
         return [d for d in order if d in wanted]
 
-    def start_round(step, c, among=DIRS):
+    def start_round(step, c, among=DIRS, when=None):
         for d in dirs_of(step):
             if d not in among:
                 continue
 
-            @pl.when(within(*d))
+            @pl.when(allowed(d, when))
             def _(d=d):
                 copy_of(step, c, d).start()
 
@@ -358,8 +372,8 @@
     def finish_round(step, c):
         settle(recv_sem.at[step % 3, c], opposite(round_sizes(step)))
 
-    def remote(a, b, recv, d):
-        @pl.when(within(*d))
+    def remote(a, b, recv, d, when=None):
+        @pl.when(allowed(d, when))
         def _():
             pltpu.make_async_remote_copy(
                 src_ref=a,
@@ -391,7 +405,7 @@
             block_send.at[:, pl.ds(0, comps)], block_recv.at[:, pl.ds(0, comps)], rim_sems.at[0], (1, 1)
         )
 
-    def start_edges(among):
+    def start_edges(among, when=None):
         for d, (first, count), to, to_row in EDGES:
             if d in among:
                 remote(
@@ -399,9 +413,10 @@
                     edge_recv.at[pl.ds(to, count), pl.ds(to_row, comps)],
                     rim_sems.at[1],
                     d,
+                    when,
                 )
 
-    def start_etas(among):
+    def start_etas(among, when=None):
         for d, slot, row, high, to, to_row in ETAS:
             if d in among:
                 remote(
@@ -409,6 +424,7 @@
                     eta_recv.at[to, pl.ds(to_row, high)],
                     rim_sems.at[1],
                     d,
+                    when,
                 )
 
     def pack_x(vals, at):
@@ -807,7 +823,10 @@
     pl.when(jnp.logical_not(soon))(answer)
     for c in range(comps):
         start_round(0, c)
+    others = tuple(d for d in DIRS if d not in FIRST and d not in LAST[2:])
+    beyond = others + LAST[2:]
     start_edges(FIRST)
+    start_edges(beyond, even)
     split_columns(n_prev)
     for c in range(comps):
         for ro in range(4):
@@ -835,32 +854,35 @@
         jnp.broadcast_to(etas[0][3:4], (8, half_y)),
     )
     start_etas(FIRST)
+    start_etas(beyond, even)
     for c in range(comps):
         apply(0, c, hold=False)
         start_round(1, c, FIRST)
-
-    @pl.when(jnp.logical_or(rad < n_rad - 1, lat < n_lat - 1))
+        start_round(1, c, beyond, even)
+
+    edge_up = jnp.logical_or(rad < n_rad - 1, lat < n_lat - 1)
+
+    @pl.when(jnp.logical_and(odd, edge_up))
     def _():
         pl.semaphore_wait(hello, around(1, LAST[:2]))
 
-    others = tuple(d for d in DIRS if d not in FIRST and d not in LAST[2:])
-    start_edges(others)
-    start_etas(others)
+    start_edges(others, odd)
+    start_etas(others, odd)
     for c in range(comps):
-        start_round(1, c, others)
+        start_round(1, c, others, odd)
 
     total = jnp.zeros((1, half_y), F32)
     prev_copy.wait()
     for i in range(n_prev):
         split_columns(i)
 
-    @pl.when(jnp.logical_and(rad < n_rad - 1, lat < n_lat - 1))
+    @pl.when(jnp.logical_and(odd, jnp.logical_and(rad < n_rad - 1, lat < n_lat - 1)))
     def _():
         pl.semaphore_wait(hello_far, 1)
 
-    start_etas(LAST[2:])
+    start_etas(LAST[2:], odd)
     for c in range(comps):
-        start_round(1, c, LAST[2:])
+        start_round(1, c, LAST[2:], odd)
     for i in range(n_prev + 1):
         total = total + gram_row(i)
 

time: 25.8 us -> 25.6 us (level)
  no operation moved by 1% of the time
where the time goes in v8:
time: 25.6 us; the launch traced here: 25.4 us
  Pallas kernels  24.8 us (97%)
  between operations  0.64 us (2%)
    pallas_call x1, Pallas kernels, on_device(): pl.pallas_call(functools.partial(kernel, n_lat, n_rad, n_steps, n_prev, c...  23.9 us
    pallas_call x1, Pallas kernels, on_device(): pl.pallas_call(store, out_shape=(jax.ShapeDtypeStruct(out.shape, F32), ja...  0.92 us

profile of v8, /device:TPU:0, one launch (start us, length us, event | category | flops | bytes accessed | tf_op | source)
XLA Modules:
  0.0 25.4 jit_solution(11131495874880588995)
XLA Ops:
  0.6 23.9 %shard_map.68 = (f32[4,192,256]{2,1,0:T(8,128)S(1)}, f32[9,9]{1,0:T(8,128)S(1)}) custom-call(f32[192,256]{1,0:T(8,128)} %bitcast.4, f32[4,192,256]{2,1,0:T(8,128)} %bitcast.3, s32[4,4,128]{2,1,0:T(4,128)} %ids_hbm.1, f32[8]{0:T(128)} %visc_hbm.1, f32[4]{0:T(128)} %shift_hbm.1), custom_call_target="tpu_custom_call" | custom-call | tf_op jit(solution)/shard_map/pallas_call | solution.py:1005
  24.5 0.9 %shard_map.69 = (f32[4,192,256]{2,1,0:T(8,128)}, f32[9,9]{1,0:T(8,128)}) custom-call(f32[4,192,256]{2,1,0:T(8,128)S(1)} %get-tuple-element.6.vec_ref, f32[9,9]{1,0:T(8,128)S(1)} %get-tuple-element.7.gram_ref), custom_call_target="tpu_custom_call" | custom-call | tf_op jit(solution)/shard_map/pallas_call | solution.py:1060

commit v9 on v7

--- a/solution.py
+++ b/solution.py
@@ -173,7 +173,7 @@
 
     for ref in (edge_recv, eta_recv):
         ref[...] = jnp.zeros_like(ref)
-    signal_around(barrier, 1, LAST)
+    signal_around(barrier, 1, DIRS)
 
     for d in DIRS:
         if d in R_DIRS:
@@ -192,20 +192,6 @@
 
     for ref in (ghost_r, ghost_x, ghost_c):
         ref[0] = jnp.zeros(ref.shape[1:], F32)
-
-    hello = token_sem.at[token_sem.shape[0] - 1]
-    hello_far = token_sem.at[token_sem.shape[0] - 2]
-
-    def answer():
-        @pl.when(jnp.logical_or(rad > 0, lat > 0))
-        def _():
-            pl.semaphore_wait(barrier, around(1, FIRST))
-
-        signal_around(hello, 1, FIRST[:2])
-        signal_around(hello_far, 1, FIRST[2:])
-
-    soon = jnp.logical_or(rad == 0, lax.rem(rad, 2) == 1)
-    pl.when(soon)(answer)
 
     reaches = []
     while (2 << len(reaches)) < max(n_lat, n_rad) - 1:
@@ -804,10 +790,10 @@
                 at = 16 * c + row
                 edge_send[2 * slot + q, c : c + 1] = edge[at : at + 1, lanes]
 
-    pl.when(jnp.logical_not(soon))(answer)
+    pl.semaphore_wait(barrier, around(1, DIRS))
     for c in range(comps):
         start_round(0, c)
-    start_edges(FIRST)
+    start_edges(DIRS)
     split_columns(n_prev)
     for c in range(comps):
         for ro in range(4):
@@ -834,33 +820,16 @@
         jnp.broadcast_to(etas[1][4:5], (8, half_y)),
         jnp.broadcast_to(etas[0][3:4], (8, half_y)),
     )
-    start_etas(FIRST)
+    start_etas(DIRS)
     for c in range(comps):
         apply(0, c, hold=False)
-        start_round(1, c, FIRST)
-
-    @pl.when(jnp.logical_or(rad < n_rad - 1, lat < n_lat - 1))
-    def _():
-        pl.semaphore_wait(hello, around(1, LAST[:2]))
-
-    others = tuple(d for d in DIRS if d not in FIRST and d not in LAST[2:])
-    start_edges(others)
-    start_etas(others)
-    for c in range(comps):
-        start_round(1, c, others)
+        start_round(1, c)
 
     total = jnp.zeros((1, half_y), F32)
     prev_copy.wait()
     for i in range(n_prev):
         split_columns(i)
 
-    @pl.when(jnp.logical_and(rad < n_rad - 1, lat < n_lat - 1))
-    def _():
-        pl.semaphore_wait(hello_far, 1)
-
-    start_etas(LAST[2:])
-    for c in range(comps):
-        start_round(1, c, LAST[2:])
     for i in range(n_prev + 1):
         total = total + gram_row(i)
 

time: 25.8 us -> 25.4 us (0.984)
  Pallas kernels: 25 us -> 24.6 us
    pallas_call x1, Pallas kernels: 24 us -> 23.7 us  [on_device(): pl.pallas_call(functools.partial(kernel, n_lat, n_rad, n_steps, n_prev, c...]
where the time goes in v9:
time: 25.4 us; the launch traced here: 25.2 us
  Pallas kernels  24.6 us (97%)
  between operations  0.64 us (3%)
    pallas_call x1, Pallas kernels, on_device(): pl.pallas_call(functools.partial(kernel, n_lat, n_rad, n_steps, n_prev, c...  23.7 us
    pallas_call x1, Pallas kernels, on_device(): pl.pallas_call(store, out_shape=(jax.ShapeDtypeStruct(out.shape, F32), ja...  0.92 us

profile of v9, /device:TPU:0, one launch (start us, length us, event | category | flops | bytes accessed | tf_op | source)
XLA Modules:
  0.0 25.2 jit_solution(6116258830265971927)
XLA Ops:
  0.6 23.7 %shard_map.68 = (f32[4,192,256]{2,1,0:T(8,128)S(1)}, f32[9,9]{1,0:T(8,128)S(1)}) custom-call(f32[192,256]{1,0:T(8,128)} %bitcast.4, f32[4,192,256]{2,1,0:T(8,128)} %bitcast.3, s32[4,4,128]{2,1,0:T(4,128)} %ids_hbm.1, f32[8]{0:T(128)} %visc_hbm.1, f32[4]{0:T(128)} %shift_hbm.1), custom_call_target="tpu_custom_call" | custom-call | tf_op jit(solution)/shard_map/pallas_call | solution.py:952
  24.3 0.9 %shard_map.69 = (f32[4,192,256]{2,1,0:T(8,128)}, f32[9,9]{1,0:T(8,128)}) custom-call(f32[4,192,256]{2,1,0:T(8,128)S(1)} %get-tuple-element.6.vec_ref, f32[9,9]{1,0:T(8,128)S(1)} %get-tuple-element.7.gram_ref), custom_call_target="tpu_custom_call" | custom-call | tf_op jit(solution)/shard_map/pallas_call | solution.py:1007

commit v10 on v9

--- a/solution.py
+++ b/solution.py
@@ -30,12 +30,12 @@
     ((1, -1), (32, 4), (4, 1), ROWS_A, 3),
     ((-1, 1), (36, 4), (3, 1), ROWS_A, 7),
 )
-EDGE_T, EDGE_U, EDGE_H, EDGE_G = 0, 4, 8, 20
+EDGE_T, EDGE_U, EDGE_H, EDGE_G = 0, 4, 8, 16
 EDGES = (
-    ((-1, -1), (8, 6), EDGE_H, 0),
-    ((-1, -1), (14, 6), EDGE_H, 4),
-    ((-1, 0), (8, 6), EDGE_H + 6, 0),
-    ((0, -1), (14, 6), EDGE_H + 6, 4),
+    ((-1, -1), (8, 4), EDGE_H, 0),
+    ((-1, -1), (12, 4), EDGE_H, 4),
+    ((-1, 0), (8, 4), EDGE_H + 4, 0),
+    ((0, -1), (12, 4), EDGE_H + 4, 4),
     ((1, 0), (0, 4), EDGE_T, 0),
     ((0, 1), (4, 4), EDGE_U, 0),
     ((1, -1), (0, 4), EDGE_G, 0),
@@ -604,8 +604,17 @@
         for g in range(2):
             t = {}
             for q in range(2):
+                near = zero
+                for c in range(comps):
+                    if g == 0:
+                        low = roll_s(ghost_c[0, c, q], c - 7)
+                        high_part = roll_s(ghost_c[0, c, q], c - 3)
+                    else:
+                        low = roll_s(ghost_r[0, c, 0, q], c - 4)
+                        high_part = roll_s(ghost_x[0, c, 0, q], c + 1)
+                    near = jnp.where(sub == c, low, jnp.where(sub == 4 + c, high_part, near))
                 t[0, 2, q], t[1, 2, q], t[2, 2, q] = forward(
-                    *(edge_recv[EDGE_H + 6 * g + 2 * n + q] for n in range(3))
+                    near, *(edge_recv[EDGE_H + 4 * g + 2 * n + q] for n in range(2))
                 )
             high.append(rim_elements(t, lambda i, g=g: rim_scaled[2 + g, i], False, True))
         for c in range(comps):
@@ -785,7 +794,7 @@
             send_r[0, c, 0, face] = edge[16 * c : 16 * c + 8, lanes]
             send_x[0, c, 0, face] = edge[16 * c + 8 : 16 * c + 16, lanes]
             send_c[0, c, 0, q : q + 1] = edge[16 * c : 16 * c + 1, lanes]
-            along = [8 + 6, 8 + 7, 3, 7, 8, 9, 10, 0, 4, 1]
+            along = [8 + 6, 8 + 7, 3, 7, 8 + 1, 8 + 2, 4, 1]
             for slot, row in enumerate(along):
                 at = 16 * c + row
                 edge_send[2 * slot + q, c : c + 1] = edge[at : at + 1, lanes]
@@ -981,8 +990,8 @@
             vmem((comps, 20) + tile, F32),
             vmem((8,) + tile, F32),
             vmem((8,) + tile, F32),
+            vmem((16,) + tile, F32),
             vmem((20,) + tile, F32),
-            vmem((24,) + tile, F32),
             vmem((3,) + tile, F32),
             vmem((4,) + tile, F32),
             vmem((4, 9) + tile, F32),

time: 25.4 us -> 25.2 us (level)
  no operation moved by 1% of the time
where the time goes in v10:
time: 25.2 us; the launch traced here: 25.1 us
  Pallas kernels  24.4 us (97%)
  between operations  0.64 us (3%)
    pallas_call x1, Pallas kernels, on_device(): pl.pallas_call(functools.partial(kernel, n_lat, n_rad, n_steps, n_prev, c...  23.5 us
    pallas_call x1, Pallas kernels, on_device(): pl.pallas_call(store, out_shape=(jax.ShapeDtypeStruct(out.shape, F32), ja...  0.92 us

profile of v10, /device:TPU:0, one launch (start us, length us, event | category | flops | bytes accessed | tf_op | source)
XLA Modules:
  0.0 25.1 jit_solution(11455818608570944403)
XLA Ops:
  0.6 23.5 %shard_map.68 = (f32[4,192,256]{2,1,0:T(8,128)S(1)}, f32[9,9]{1,0:T(8,128)S(1)}) custom-call(f32[192,256]{1,0:T(8,128)} %bitcast.4, f32[4,192,256]{2,1,0:T(8,128)} %bitcast.3, s32[4,4,128]{2,1,0:T(4,128)} %ids_hbm.1, f32[8]{0:T(128)} %visc_hbm.1, f32[4]{0:T(128)} %shift_hbm.1), custom_call_target="tpu_custom_call" | custom-call | tf_op jit(solution)/shard_map/pallas_call | solution.py:961
  24.2 0.9 %shard_map.69 = (f32[4,192,256]{2,1,0:T(8,128)}, f32[9,9]{1,0:T(8,128)}) custom-call(f32[4,192,256]{2,1,0:T(8,128)S(1)} %get-tuple-element.6.vec_ref, f32[9,9]{1,0:T(8,128)S(1)} %get-tuple-element.7.gram_ref), custom_call_target="tpu_custom_call" | custom-call | tf_op jit(solution)/shard_map/pallas_call | solution.py:1016

commit v11 on v10

--- a/solution.py
+++ b/solution.py
@@ -935,8 +935,7 @@
 
 def store(vec_ref, gram_ref, vec_out, gram_out, sems):
     copies = [pltpu.make_async_copy(gram_ref, gram_out, sems.at[0])]
-    for i in range(vec_ref.shape[0]):
-        copies.append(pltpu.make_async_copy(vec_ref.at[i], vec_out.at[i], sems.at[1 + i]))
+    copies.insert(0, pltpu.make_async_copy(vec_ref, vec_out, sems.at[1]))
     for copy in copies:
         copy.start()
     for copy in copies:
@@ -1021,7 +1020,7 @@
         ),
         in_specs=[vmem_spec] * 2,
         out_specs=(hbm_spec, hbm_spec),
-        scratch_shapes=[pltpu.SemaphoreType.DMA((1 + n_steps,))],
+        scratch_shapes=[pltpu.SemaphoreType.DMA((2,))],
     )(*(pltpu.with_memory_space_constraint(a, pltpu.VMEM) for a in (out, gram)))
     return out.reshape((n_steps,) + residual.shape), gram
 

time: 25.2 us -> 25.2 us (level)
  no operation moved by 1% of the time
where the time goes in v11:
time: 25.2 us; the launch traced here: 25.1 us
  Pallas kernels  24.4 us (97%)
  between operations  0.64 us (3%)
    pallas_call x1, Pallas kernels, on_device(): pl.pallas_call(functools.partial(kernel, n_lat, n_rad, n_steps, n_prev, c...  23.5 us
    pallas_call x1, Pallas kernels, on_device(): pl.pallas_call(store, out_shape=(jax.ShapeDtypeStruct(out.shape, F32), ja...  0.9 us

profile of v11, /device:TPU:0, one launch (start us, length us, event | category | flops | bytes accessed | tf_op | source)
XLA Modules:
  0.0 25.1 jit_solution(11669006220543023790)
XLA Ops:
  0.6 23.5 %shard_map.68 = (f32[4,192,256]{2,1,0:T(8,128)S(1)}, f32[9,9]{1,0:T(8,128)S(1)}) custom-call(f32[192,256]{1,0:T(8,128)} %bitcast.4, f32[4,192,256]{2,1,0:T(8,128)} %bitcast.3, s32[4,4,128]{2,1,0:T(4,128)} %ids_hbm.1, f32[8]{0:T(128)} %visc_hbm.1, f32[4]{0:T(128)} %shift_hbm.1), custom_call_target="tpu_custom_call" | custom-call | tf_op jit(solution)/shard_map/pallas_call | solution.py:960
  24.2 0.9 %shard_map.69 = (f32[4,192,256]{2,1,0:T(8,128)}, f32[9,9]{1,0:T(8,128)}) custom-call(f32[4,192,256]{2,1,0:T(8,128)S(1)} %get-tuple-element.6.vec_ref, f32[9,9]{1,0:T(8,128)S(1)} %get-tuple-element.7.gram_ref), custom_call_target="tpu_custom_call" | custom-call | tf_op jit(solution)/shard_map/pallas_call | solution.py:1015
